TPU v7x, 32 devices: a 4x4x1 block of a 4x4x8 slice. The times are simulated.
32 devices in a mesh: dp: 1 (over z), sub: 4 (over y), ep: 8 (over x, core).
Axes of the slice: x: 4, y: 4, z: 1, core: 2. Of those that a mesh axis runs over, the one named last changes fastest.
The devices are a block of a 4x4x8 slice.
Arguments:
- input_a: bfloat16 [32, 512, 2048], P(('dp', 'ep', 'sub'))
- input_b: bfloat16 [32, 512, 2048], P(('dp', 'ep', 'sub'))
- route_idx: int32 [2, 16384, 8], P(None, ('dp', 'ep', 'sub'))
- route_gate: float32 [2, 16384, 8], P(None, ('dp', 'ep', 'sub'))
- attn_norm: float32 [2048], replicated
- w_query: bfloat16 [2048, 32, 128], replicated
- w_key: bfloat16 [2048, 32, 128], replicated
- w_value: bfloat16 [2048, 32, 128], replicated
- w_out: bfloat16 [32, 128, 2048], replicated
- moe_norm: float32 [2048], replicated
- w_gate: bfloat16 [128, 2048, 768], P(('ep', 'sub'))
- w_up: bfloat16 [128, 2048, 768], P(('ep', 'sub'))
- w_down: bfloat16 [128, 768, 2048], P(('ep', 'sub'))
Outputs:
- output 1: bfloat16 [32, 512, 2048], P(('dp', 'ep', 'sub'))
- output 2: bfloat16 [32, 512, 2048], P(('dp', 'ep', 'sub'))
All inputs are finite; a program needn't handle non-finite values.
Results may differ from a plain program's by a relative error of at most 0.0126963.
Values are sent between devices in bfloat16 or wider.
A program may use at most 768 MiB of HBM per device.

v0:
```python
import jax
import jax.numpy as jnp
from jax import lax
from jax.sharding import PartitionSpec as P

NORM_EPS = 1e-6


def rms_norm(values, norm_gain):
    acc_f32 = values.astype(jnp.float32)
    inv_rms = lax.rsqrt(jnp.mean(acc_f32 * acc_f32, axis=-1, keepdims=True) + NORM_EPS)
    return (acc_f32 * inv_rms * norm_gain).astype(jnp.bfloat16)


def attention_block(tokens, attn_norm, w_query, w_key, w_value, w_out):
    normed = rms_norm(tokens, attn_norm)
    q_heads = jnp.einsum('bsd,dhc->bshc', normed, w_query, preferred_element_type=jnp.float32).astype(jnp.bfloat16)
    k_heads = jnp.einsum('bsd,dhc->bshc', normed, w_key, preferred_element_type=jnp.float32).astype(jnp.bfloat16)
    v_heads = jnp.einsum('bsd,dhc->bshc', normed, w_value, preferred_element_type=jnp.float32).astype(jnp.bfloat16)
    score_scale = w_query.shape[2] ** -0.5
    scores = jnp.einsum('bqhc,bkhc->bhqk', q_heads, k_heads, preferred_element_type=jnp.float32) * score_scale
    seq_len = tokens.shape[1]
    causal = lax.broadcasted_iota(jnp.int32, (seq_len, seq_len), 0) >= lax.broadcasted_iota(jnp.int32, (seq_len, seq_len), 1)
    scores = jnp.where(causal, scores, -jnp.inf)
    prob_bf = jax.nn.softmax(scores, axis=-1).astype(jnp.bfloat16)
    context = jnp.einsum('bhqk,bkhc->bqhc', prob_bf, v_heads, preferred_element_type=jnp.float32).astype(jnp.bfloat16)
    proj_out = jnp.einsum('crid,ide->cre', context, w_out, preferred_element_type=jnp.float32)
    return (tokens.astype(jnp.float32) + proj_out).astype(jnp.bfloat16)


def route_slots(exp_ids, num_exp, cap_slots):
    tok_count, top_k = exp_ids.shape
    flat_ids = exp_ids.reshape(-1)
    sort_order = jnp.argsort(flat_ids, stable=True)
    sorted_ids = flat_ids[sort_order]
    counts = jnp.bincount(flat_ids, length=num_exp)
    starts = jnp.cumsum(counts) - counts
    slot_rank = jnp.arange(flat_ids.shape[0], dtype=jnp.int32) - starts[sorted_ids]
    slot_sorted = sorted_ids * cap_slots + slot_rank
    slot_of = jnp.zeros_like(flat_ids).at[sort_order].set(slot_sorted)
    holder = jnp.full((num_exp * cap_slots,), tok_count, jnp.int32).at[slot_sorted].set(sort_order // top_k)
    return slot_of, holder


def expert_ffn(disp_rows, w_gate, w_up, w_down):
    gate_h = jnp.einsum('end,edf->enf', disp_rows, w_gate, preferred_element_type=jnp.float32)
    up_h = jnp.einsum('end,edf->enf', disp_rows, w_up, preferred_element_type=jnp.float32)
    act_rows = (jax.nn.silu(gate_h) * up_h).astype(jnp.bfloat16)
    return jnp.einsum('enf,efd->end', act_rows, w_down, preferred_element_type=jnp.float32).astype(jnp.bfloat16)


def micro_step(tokens, exp_ids, gate_w, attn_norm, w_query, w_key, w_value, w_out, moe_norm, w_gate, w_up, w_down, ep_size, sub_size):
    hidden = attention_block(tokens, attn_norm, w_query, w_key, w_value, w_out)
    seq_count, seq_len, model_dim = hidden.shape
    flat_tok = hidden.reshape(seq_count * seq_len, model_dim)
    tok_count, top_k = exp_ids.shape
    exp_local = w_gate.shape[0]
    num_exp = exp_local * ep_size * sub_size
    cap_slots = 3 * top_k * tok_count // (2 * num_exp)
    normed = rms_norm(flat_tok, moe_norm)
    slot_of, holder = route_slots(exp_ids, num_exp, cap_slots)
    send_buf = jnp.take(normed, holder, axis=0, mode='fill', fill_value=0)
    send_buf = send_buf.reshape(ep_size, sub_size, exp_local, cap_slots, model_dim)
    across_ep = lax.all_to_all(send_buf, 'ep', 0, 3, tiled=True)
    arrived = lax.all_to_all(across_ep, 'sub', 1, 3, tiled=True)
    expert_out = expert_ffn(arrived.reshape(exp_local, -1, model_dim), w_gate, w_up, w_down)
    back_sub = lax.all_to_all(expert_out.reshape(1, 1, exp_local, -1, model_dim), 'sub', 3, 1, tiled=True)
    returned = lax.all_to_all(back_sub, 'ep', 3, 0, tiled=True)
    picked = jnp.take(returned.reshape(num_exp * cap_slots, model_dim), slot_of, axis=0).reshape(tok_count, top_k, model_dim)
    moe_sum = jnp.sum(gate_w[:, :, None] * picked.astype(jnp.float32), axis=1)
    out_tok = (flat_tok.astype(jnp.float32) + moe_sum).astype(jnp.bfloat16)
    return out_tok.reshape(seq_count, seq_len, model_dim)


def solution(mesh):
    ep_size = mesh.shape['ep']
    sub_size = mesh.shape['sub']
    tok_spec = P(('dp', 'ep', 'sub'), None, None)
    route_spec = P(None, ('dp', 'ep', 'sub'), None)
    exp_spec = P(('ep', 'sub'), None, None)

    def device_body(input_a, input_b, route_idx, route_gate, attn_norm, w_query, w_key, w_value, w_out, moe_norm, w_gate, w_up, w_down):
        out_a = micro_step(input_a, route_idx[0], route_gate[0], attn_norm, w_query, w_key, w_value, w_out, moe_norm, w_gate, w_up, w_down, ep_size, sub_size)
        out_b = micro_step(input_b, route_idx[1], route_gate[1], attn_norm, w_query, w_key, w_value, w_out, moe_norm, w_gate, w_up, w_down, ep_size, sub_size)
        return out_a, out_b

    return jax.shard_map(device_body, mesh=mesh, in_specs=(tok_spec, tok_spec, route_spec, route_spec, P(), P(), P(), P(), P(), P(), exp_spec, exp_spec, exp_spec), out_specs=(tok_spec, tok_spec), check_vma=False)
```

profile of v0, /device:TPU:97, one launch (start us, length us, event | category | flops | bytes accessed | tf_op | source)
XLA Modules:
  0.0 2733.5 jit_solution(2517946955651804647)
XLA Ops:
  2.4 5.8 sort.32
  8.8 23.0 gather_fusion.2
  32.2 28.8 %scatter_custom_fusion.3 = s32[128]{0:T(128)S(1)} fusion(s32[4096]{0:T(1024)S(1)} %reshape.462, s32[4096]{0:T(1024)S(1)} %broadcast.234, s32[]{:T(128)} %constant.74.clone.1), kind=kCustom, calls=%fused_computation.161 | custom fusion | flops 4096 | bytes 516 | tf_op jit(solution)/shard_map/scatter-add | solution.py:36
  61.4 24.7 gather_fusion.3
  86.7 15.5 scatter_custom_fusion.4
  103.9 2.1 fusion.40
  106.1 14.6 fusion.20
  120.7 14.0 fusion.22
  134.7 22.8 fusion.53
  157.5 23.7 fusion.66
  181.2 34.1 %fusion.120 = (f32[32,512]{1,0:T(8,128)S(1)}, f32[32,512,512]{1,2,0:T(8,128)}) fusion(f32[32,512,512]{1,2,0:T(8,128)} %fusion.53, pred[512,512]{0,1:T(8,128)(4,1)S(1)} %iota_compare_fusion), kind=kOutput, calls=%fused_computation.169 | output fusion | flops 50332160 | bytes 67436544 | tf_op jit(solution)/shard_map/sub | solution.py:25
  215.3 34.1 %fusion.119 = (f32[32,512]{1,0:T(8,128)S(1)}, f32[32,512,512]{1,2,0:T(8,128)}) fusion(f32[32,512,512]{1,2,0:T(8,128)} %fusion.66, pred[512,512]{0,1:T(8,128)(4,1)S(1)} %iota_compare_fusion), kind=kOutput, calls=%fused_computation.168 | output fusion | flops 50332160 | bytes 67436544 | tf_op jit(solution)/shard_map/sub | solution.py:25
  249.4 21.5 fusion.13
  270.9 14.8 fusion.36
  285.7 22.0 fusion.12
  307.7 14.5 fusion.32
  323.5 2.2 fusion.38
  325.8 48.2 %gather_fusion.6 = bf16[6144,2048]{1,0:T(8,128)(2,1)} fusion(bf16[512,2048]{1,0:T(8,128)(2,1)} %get-tuple-element.20, s32[6144]{0:T(1024)S(1)} %copy-done.15), kind=kCustom, calls=%fused_computation.2.clone | custom fusion | bytes 50356224 | tf_op jit(solution)/shard_map/jit(_take)/gather | solution.py:62
  374.0 21.6 broadcast_select_fusion
  395.5 8.5 all-to-all-start.4
  404.3 5.8 sort.31
  410.7 23.0 gather_fusion
  434.0 29.0 %scatter_custom_fusion = s32[128]{0:T(128)S(1)} fusion(s32[4096]{0:T(1024)S(1)} %reshape.438, s32[4096]{0:T(1024)} %copy-done.20, s32[]{:T(128)} %constant.74.clone.1), kind=kCustom, calls=%fused_computation.163 | custom fusion | flops 4096 | bytes 1024 | tf_op jit(solution)/shard_map/scatter-add | solution.py:36
  463.4 24.7 gather_fusion.1
  488.8 15.5 scatter_custom_fusion.1
  504.3 31.1 %gather_fusion.4 = bf16[6144,2048]{1,0:T(8,128)(2,1)} fusion(bf16[512,2048]{1,0:T(8,128)(2,1)S(1)} %get-tuple-element.21, s32[6144]{0:T(1024)S(1)} %fusion.84), kind=kCustom, calls=%fused_computation.clone | custom fusion | bytes 50356224 | tf_op jit(solution)/shard_map/jit(_take)/gather | solution.py:62
  535.5 21.6 broadcast_select_fusion.1
  557.1 120.3 %all-to-all-done.4 = bf16[8,4,4,48,2048]{4,3,2,1,0:T(8,128)(2,1)} async-done(((bf16[8,4,4,48,2048]{4,3,2,1,0:T(8,128)(2,1)}), bf16[8,4,4,48,2048]{4,3,2,1,0:T(8,128)(2,1)}, u32[]{:S(2)}, u32[]{:S(2)}) %all-to-all-start.4) | async-done | bytes 25165856 | tf_op jit(solution)/shard_map/all_to_all | solution.py:64
  677.4 7.3 all-to-all-start
  684.7 21.1 copy.68
  705.8 252.3 %all-to-all-done = bf16[8,4,4,48,2048]{4,3,2,1,0:T(8,128)(2,1)} async-done(((bf16[8,4,4,48,2048]{4,3,2,1,0:T(8,128)(2,1)}), bf16[8,4,4,48,2048]{4,3,2,1,0:T(8,128)(2,1)}, u32[]{:S(2)}, u32[]{:S(2)}) %all-to-all-start) | async-done | bytes 25165856 | tf_op jit(solution)/shard_map/all_to_all | solution.py:64
  958.1 8.6 all-to-all-start.5
  966.7 21.0 copy.53
  987.8 252.1 %all-to-all-done.5 = bf16[1,4,4,384,2048]{4,3,2,0,1:T(8,128)(2,1)} async-done(((bf16[1,4,4,384,2048]{4,3,2,0,1:T(8,128)(2,1)}), bf16[1,4,4,384,2048]{4,3,2,0,1:T(8,128)(2,1)}, u32[]{:S(2)}, u32[]{:S(2)}) %all-to-all-start.5) | async-done | bytes 25165856 | tf_op jit(solution)/shard_map/all_to_all | solution.py:65
  1239.9 8.5 all-to-all-start.1
  1248.4 21.0 copy.69
  1269.4 28.7 %fusion.122 = f32[4,1536,768]{2,1,0:T(8,128)} fusion(bf16[4,1536,2048]{2,1,0:T(8,128)(2,1)} %bitcast.190, bf16[4,2048,768]{2,1,0:T(8,128)(2,1)} %param.27), kind=kOutput, calls=%fused_computation.171 | convolution fusion | flops 19327352832 | bytes 56623104 | tf_op jit(solution)/shard_map/end,edf->enf/dot_general | solution.py:46
  1298.1 31.1 %fusion.168 = bf16[4,1536,768]{2,1,0:T(8,128)(2,1)} fusion(bf16[4,2048,768]{2,1,0:T(8,128)(2,1)} %param.28, bf16[4,1536,2048]{2,1,0:T(8,128)(2,1)} %bitcast.191, f32[4,1536,768]{2,1,0:T(8,128)} %fusion.122), kind=kOutput, calls=%bitcast_fusion.1.clone | convolution fusion | flops 19355664384 | bytes 66060288 | tf_op jit(solution)/shard_map/end,edf->enf/dot_general | solution.py:47
  1329.3 29.2 %fusion.7 = bf16[1,1,4,1536,2048]{4,3,2,1,0:T(8,128)(2,1)} fusion(bf16[4,768,2048]{2,1,0:T(8,128)(2,1)} %param.29, bf16[4,1536,768]{2,1,0:T(8,128)(2,1)} %fusion.168), kind=kOutput, calls=%fused_computation.35 | convolution fusion | flops 19339935744 | bytes 47185920 | tf_op jit(solution)/shard_map/enf,efd->end/dot_general | solution.py:49
  1358.5 32.1 %copy.70 = bf16[1,1,4,1536,2048]{4,2,1,0,3:T(4,128)(2,1)} copy(bf16[1,1,4,1536,2048]{4,3,2,1,0:T(8,128)(2,1)} %fusion.7) | data formatting | bytes 50331648 | tf_op jit(solution)/shard_map/reshape | solution.py:67
  1390.6 129.4 %all-to-all-done.1 = bf16[1,4,4,384,2048]{4,3,2,0,1:T(8,128)(2,1)} async-done(((bf16[1,4,4,384,2048]{4,3,2,0,1:T(8,128)(2,1)}), bf16[1,4,4,384,2048]{4,3,2,0,1:T(8,128)(2,1)}, u32[]{:S(2)}, u32[]{:S(2)}) %all-to-all-start.1) | async-done | bytes 25165856 | tf_op jit(solution)/shard_map/all_to_all | solution.py:65
  1520.1 9.0 all-to-all-start.6
  1529.0 21.1 copy.54
  1550.1 28.8 %fusion.121 = f32[4,1536,768]{2,1,0:T(8,128)} fusion(bf16[4,1536,2048]{2,1,0:T(8,128)(2,1)} %bitcast.192, bf16[4,2048,768]{2,1,0:T(8,128)(2,1)} %param.27), kind=kOutput, calls=%fused_computation.170 | convolution fusion | flops 19327352832 | bytes 56623104 | tf_op jit(solution)/shard_map/end,edf->enf/dot_general | solution.py:46
  1578.9 31.1 %fusion.164 = bf16[4,1536,768]{2,1,0:T(8,128)(2,1)} fusion(bf16[4,2048,768]{2,1,0:T(8,128)(2,1)} %param.28, bf16[4,1536,2048]{2,1,0:T(8,128)(2,1)} %bitcast.193, f32[4,1536,768]{2,1,0:T(8,128)} %fusion.121), kind=kOutput, calls=%bitcast_fusion.clone.1 | convolution fusion | flops 19355664384 | bytes 66060288 | tf_op jit(solution)/shard_map/end,edf->enf/dot_general | solution.py:47
  1610.0 29.2 %fusion.6 = bf16[1,1,4,1536,2048]{4,3,2,1,0:T(8,128)(2,1)} fusion(bf16[4,768,2048]{2,1,0:T(8,128)(2,1)} %param.29, bf16[4,1536,768]{2,1,0:T(8,128)(2,1)} %fusion.164), kind=kOutput, calls=%fused_computation.34 | convolution fusion | flops 19339935744 | bytes 47185920 | tf_op jit(solution)/shard_map/enf,efd->end/dot_general | solution.py:49
  1639.2 32.1 %copy.55 = bf16[1,1,4,1536,2048]{4,2,1,0,3:T(4,128)(2,1)} copy(bf16[1,1,4,1536,2048]{4,3,2,1,0:T(8,128)(2,1)} %fusion.6) | data formatting | bytes 50331648 | tf_op jit(solution)/shard_map/reshape | solution.py:67
  1671.3 128.4 %all-to-all-done.6 = bf16[1,1,4,1536,2048]{4,2,1,0,3:T(4,128)(2,1)} async-done(((bf16[1,1,4,1536,2048]{4,2,1,0,3:T(4,128)(2,1)}), bf16[1,1,4,1536,2048]{4,2,1,0,3:T(4,128)(2,1)}, u32[]{:S(2)}, u32[]{:S(2)}) %all-to-all-start.6) | async-done | bytes 25165856 | tf_op jit(solution)/shard_map/all_to_all | solution.py:67
  1799.7 8.6 all-to-all-start.2
  1808.3 30.6 %copy.109 = bf16[1,1,4,4,384,2048]{5,3,2,4,1,0:T(4,128)(2,1)} copy(bf16[1,1,4,4,384,2048]{5,2,4,3,1,0:T(4,128)(2,1)} %bitcast.52) | data formatting | bytes 50331648 | tf_op jit(solution)/shard_map/all_to_all | solution.py:67
  1838.9 239.1 %all-to-all-done.2 = bf16[1,1,4,1536,2048]{4,2,1,0,3:T(4,128)(2,1)} async-done(((bf16[1,1,4,1536,2048]{4,2,1,0,3:T(4,128)(2,1)}), bf16[1,1,4,1536,2048]{4,2,1,0,3:T(4,128)(2,1)}, u32[]{:S(2)}, u32[]{:S(2)}) %all-to-all-start.2) | async-done | bytes 25165856 | tf_op jit(solution)/shard_map/all_to_all | solution.py:67
  2078.0 11.0 all-to-all-start.7
  2089.0 30.6 %copy.110 = bf16[1,1,4,4,384,2048]{5,3,2,4,1,0:T(4,128)(2,1)} copy(bf16[1,1,4,4,384,2048]{5,2,4,3,1,0:T(4,128)(2,1)} %bitcast.22) | data formatting | bytes 50331648 | tf_op jit(solution)/shard_map/all_to_all | solution.py:67
  2119.5 242.8 %all-to-all-done.7 = bf16[1,4,4,384,2048]{4,1,2,0,3:T(4,128)(2,1)} async-done(((bf16[1,4,4,384,2048]{4,1,2,0,3:T(4,128)(2,1)}), bf16[1,4,4,384,2048]{4,1,2,0,3:T(4,128)(2,1)}, u32[]{:S(2)}, u32[]{:S(2)}) %all-to-all-start.7) | async-done | bytes 25165856 | tf_op jit(solution)/shard_map/all_to_all | solution.py:68
  2362.4 7.6 all-to-all-start.3
  2370.3 15.7 scatter_custom_fusion.5
  2386.0 15.9 scatter_custom_fusion.2
  2402.0 26.9 copy.72
  2428.9 42.7 %gather_fusion.7 = bf16[4096,2048]{1,0:T(8,128)(2,1)} fusion(bf16[6144,2048]{1,0:T(8,128)(2,1)} %bitcast.182, s32[4096]{0:T(1024)S(1)} %fusion.91), kind=kCustom, calls=%fused_computation.3.clone | custom fusion | bytes 33570816 | tf_op jit(solution)/shard_map/jit(_take)/gather | solution.py:69
  2471.6 17.8 fusion.2
  2491.4 152.0 %all-to-all-done.3 = bf16[1,4,4,384,2048]{4,1,2,0,3:T(4,128)(2,1)} async-done(((bf16[1,4,4,384,2048]{4,1,2,0,3:T(4,128)(2,1)}), bf16[1,4,4,384,2048]{4,1,2,0,3:T(4,128)(2,1)}, u32[]{:S(2)}, u32[]{:S(2)}) %all-to-all-start.3) | async-done | bytes 25165856 | tf_op jit(solution)/shard_map/all_to_all | solution.py:68
  2643.4 27.1 copy.57
  2670.4 42.7 %gather_fusion.5 = bf16[4096,2048]{1,0:T(8,128)(2,1)} fusion(bf16[6144,2048]{1,0:T(8,128)(2,1)} %bitcast.183, s32[4096]{0:T(1024)S(1)} %fusion.90), kind=kCustom, calls=%fused_computation.1.clone | custom fusion | bytes 33570816 | tf_op jit(solution)/shard_map/jit(_take)/gather | solution.py:69
  2713.2 17.8 fusion.3
  (94 shorter events, 13.3 us)
Async XLA Ops:
  31.8 88.9 %copy-start.7 = (s32[4096]{0:T(1024)}, s32[4096]{0:T(1024)S(1)}, u32[]{:S(2)}) copy-start(s32[4096]{0:T(1024)S(1)} %gather_fusion.2) | copy-start | bytes 49156
  31.8 71.7 %copy-start.4 = (bf16[1,512,2048]{2,1,0:T(8,128)(2,1)S(1)}, bf16[1,512,2048]{2,1,0:T(8,128)(2,1)}, u32[]{:S(2)}) copy-start(bf16[1,512,2048]{2,1,0:T(8,128)(2,1)} %param.18) | copy-start | bytes 6291460
  31.8 74.2 %copy-start.22 = (f32[2048]{0:T(1024)S(1)}, f32[2048]{0:T(1024)}, u32[]{:S(2)}) copy-start(f32[2048]{0:T(1024)} %param.21) | copy-start | bytes 24580
  32.2 28.8 %copy-start.20 = (s32[4096]{0:T(1024)}, s32[4096]{0:T(1024)S(1)}, u32[]{:S(2)}) copy-start(s32[4096]{0:T(1024)S(1)} %broadcast.234) | copy-start | bytes 49156
  86.1 0.6 copy-start.11
  106.0 14.6 copy-start.5
  285.7 22.0 copy-start.6
  307.7 15.8 copy-start.2
  307.7 15.8 copy-start.21
  307.7 18.1 copy-start.15
  322.2 1.3 copy-start
  325.8 48.2 %copy-start.19 = (pred[6144]{0:T(1024)(128)(4,1)S(1)}, pred[6144]{0:T(1024)(128)(4,1)}, u32[]{:S(2)}) copy-start(pred[6144]{0:T(1024)(128)(4,1)} %compare_and_fusion) | copy-start | bytes 18436
  395.5 8.5 copy-start.17
  395.5 281.9 %all-to-all-start.4 = ((bf16[8,4,4,48,2048]{4,3,2,1,0:T(8,128)(2,1)}), bf16[8,4,4,48,2048]{4,3,2,1,0:T(8,128)(2,1)}, u32[]{:S(2)}, u32[]{:S(2)}) async-start(bf16[8,4,4,48,2048]{4,3,2,1,0:T(8,128)(2,1)} %bitcast.184), calls=%async_computation.4 | async-start | bytes 50331648 | tf_op jit(solution)/shard_map/all_to_all | solution.py:64
  404.0 29.7 %copy-start.16 = (s32[1,512,8]{1,2,0:T(8,128)S(1)}, s32[1,512,8]{1,2,0:T(8,128)}, u32[]{:S(2)}) copy-start(s32[1,512,8]{1,2,0:T(8,128)} %get-tuple-element.11) | copy-start | bytes 49156
  433.7 101.7 %copy-start.9 = (s32[4096]{0:T(1024)}, s32[4096]{0:T(1024)S(1)}, u32[]{:S(2)}) copy-start(s32[4096]{0:T(1024)S(1)} %gather_fusion) | copy-start | bytes 49156
  488.2 0.6 copy-start.13
  677.4 280.7 %all-to-all-start = ((bf16[8,4,4,48,2048]{4,3,2,1,0:T(8,128)(2,1)}), bf16[8,4,4,48,2048]{4,3,2,1,0:T(8,128)(2,1)}, u32[]{:S(2)}, u32[]{:S(2)}) async-start(bf16[8,4,4,48,2048]{4,3,2,1,0:T(8,128)(2,1)} %bitcast.187), calls=%async_computation | async-start | bytes 50331648 | tf_op jit(solution)/shard_map/all_to_all | solution.py:64
  958.1 281.8 %all-to-all-start.5 = ((bf16[1,4,4,384,2048]{4,3,2,0,1:T(8,128)(2,1)}), bf16[1,4,4,384,2048]{4,3,2,0,1:T(8,128)(2,1)}, u32[]{:S(2)}, u32[]{:S(2)}) async-start(bf16[1,4,4,384,2048]{4,3,2,0,1:T(8,128)(2,1)} %bitcast.188), calls=%async_computation.5 | async-start | bytes 50331648 | tf_op jit(solution)/shard_map/all_to_all | solution.py:65
  1239.9 280.2 %all-to-all-start.1 = ((bf16[1,4,4,384,2048]{4,3,2,0,1:T(8,128)(2,1)}), bf16[1,4,4,384,2048]{4,3,2,0,1:T(8,128)(2,1)}, u32[]{:S(2)}, u32[]{:S(2)}) async-start(bf16[1,4,4,384,2048]{4,3,2,0,1:T(8,128)(2,1)} %bitcast.186), calls=%async_computation.1 | async-start | bytes 50331648 | tf_op jit(solution)/shard_map/all_to_all | solution.py:65
  1520.1 279.6 %all-to-all-start.6 = ((bf16[1,1,4,1536,2048]{4,2,1,0,3:T(4,128)(2,1)}), bf16[1,1,4,1536,2048]{4,2,1,0,3:T(4,128)(2,1)}, u32[]{:S(2)}, u32[]{:S(2)}) async-start(bf16[1,1,4,1536,2048]{4,2,1,0,3:T(4,128)(2,1)} %copy.70), calls=%async_computation.6 | async-start | bytes 50331648 | tf_op jit(solution)/shard_map/all_to_all | solution.py:67
  1799.7 278.3 %all-to-all-start.2 = ((bf16[1,1,4,1536,2048]{4,2,1,0,3:T(4,128)(2,1)}), bf16[1,1,4,1536,2048]{4,2,1,0,3:T(4,128)(2,1)}, u32[]{:S(2)}, u32[]{:S(2)}) async-start(bf16[1,1,4,1536,2048]{4,2,1,0,3:T(4,128)(2,1)} %copy.55), calls=%async_computation.2 | async-start | bytes 50331648 | tf_op jit(solution)/shard_map/all_to_all | solution.py:67
  2078.0 284.3 %all-to-all-start.7 = ((bf16[1,4,4,384,2048]{4,1,2,0,3:T(4,128)(2,1)}), bf16[1,4,4,384,2048]{4,1,2,0,3:T(4,128)(2,1)}, u32[]{:S(2)}, u32[]{:S(2)}) async-start(bf16[1,4,4,384,2048]{4,1,2,0,3:T(4,128)(2,1)} %bitcast.189), calls=%async_computation.7 | async-start | bytes 50331648 | tf_op jit(solution)/shard_map/all_to_all | solution.py:68
  2362.3 7.7 copy-start.18
  2362.3 7.9 copy-start.8
  2362.4 7.9 copy-start.12
  2362.4 23.6 copy-start.10
  2362.4 23.6 copy-start.14
  2362.4 281.0 %all-to-all-start.3 = ((bf16[1,4,4,384,2048]{4,1,2,0,3:T(4,128)(2,1)}), bf16[1,4,4,384,2048]{4,1,2,0,3:T(4,128)(2,1)}, u32[]{:S(2)}, u32[]{:S(2)}) async-start(bf16[1,4,4,384,2048]{4,1,2,0,3:T(4,128)(2,1)} %bitcast.185), calls=%async_computation.3 | async-start | bytes 50331648 | tf_op jit(solution)/shard_map/all_to_all | solution.py:68
  2471.6 17.8 copy-start.3
  2713.2 17.8 copy-start.1
where the time goes:
time: 2740 us; the launch traced here: 2730 us
  waiting for transfers between devices  1520 us (55%)
  local copies, waits for them, and re-layouts  590 us (22%)
  matrix products  326 us (12%)
  other arithmetic  230 us (8%)
  starting transfers between devices  69.1 us (3%)
    all_to_all x2, waiting for transfers between devices, micro_step(): returned = lax.all_to_all(back_sub, 'ep', 3, 0, tiled=True)  395 us
    all_to_all x2, waiting for transfers between devices, micro_step(): arrived = lax.all_to_all(across_ep, 'sub', 1, 3, tiled=True)  382 us
    all_to_all x2, waiting for transfers between devices, micro_step(): across_ep = lax.all_to_all(send_buf, 'ep', 0, 3, tiled=True)  373 us
    all_to_all x2, waiting for transfers between devices, micro_step(): lax.all_to_all(expert_out.reshape(1, 1, exp_local, -1, model_dim), 'sub',...  367 us
    gather x2, local copies, waits for them, and re-layouts, micro_step(): jnp.take(returned.reshape(num_exp * cap_slots, model_dim), slot_of, axis=0)  85.4 us
    gather x2, local copies, waits for them, and re-layouts, micro_step(): send_buf = jnp.take(normed, holder, axis=0, mode='fill', fill_value=0)  79.3 us
    sub x2, other arithmetic, attention_block(): prob_bf = jax.nn.softmax(scores, axis=-1).astype(jnp.bfloat16)  68.2 us
    reshape x2, local copies, waits for them, and re-layouts, micro_step(): expert_out.reshape(1, 1, exp_local, -1, model_dim)  64.2 us
  transfers between devices with their start and end apart: 8, of which 8 were waited for; matrix products, arithmetic and copies ran while one was open for 24% of the time, Pallas kernels for 0%

commit v1 on v0

v1 whole, which is shorter than its diff:
```python
import functools

import jax
import jax.numpy as jnp
from jax import lax
from jax.experimental import pallas as pl
from jax.experimental.pallas import tpu as pltpu
from jax.sharding import PartitionSpec as P

NORM_EPS = 1e-6
VMEM_MAX = 60 * 1024 * 1024
F32 = jnp.float32
BF16 = jnp.bfloat16


def rms_norm(values, norm_gain):
    acc_f32 = values.astype(F32)
    inv_rms = lax.rsqrt(jnp.mean(acc_f32 * acc_f32, axis=-1, keepdims=True) + NORM_EPS)
    return (acc_f32 * inv_rms * norm_gain).astype(BF16)


def attn_kernel(scale, q_ref, k_ref, v_ref, o_ref):
    heads, seq_len, head_dim = q_ref.shape
    half = seq_len // 2
    for h in range(heads):
        for part in range(2):
            keys = (part + 1) * half
            q = q_ref[h, part * half:keys, :]
            k = k_ref[h, :keys, :]
            s = lax.dot_general(q, k, (((1,), (1,)), ((), ())), preferred_element_type=F32) * scale
            rows = lax.broadcasted_iota(jnp.int32, s.shape, 0) + part * half
            cols = lax.broadcasted_iota(jnp.int32, s.shape, 1)
            s = jnp.where(rows >= cols, s, -jnp.inf)
            p = jnp.exp(s - jnp.max(s, axis=-1, keepdims=True))
            p = (p / jnp.sum(p, axis=-1, keepdims=True)).astype(BF16)
            o = jnp.dot(p, v_ref[h, :keys, :], preferred_element_type=F32)
            o_ref[part * half:keys, h * head_dim:(h + 1) * head_dim] = o.astype(BF16)


def attention_core(q, k, v):
    heads, seq_len, head_dim = q.shape
    step = 4
    spec = pl.BlockSpec((step, seq_len, head_dim), lambda i: (i, 0, 0))
    return pl.pallas_call(
        functools.partial(attn_kernel, head_dim ** -0.5),
        grid=(heads // step,),
        out_shape=jax.ShapeDtypeStruct((seq_len, heads * head_dim), BF16),
        in_specs=[spec, spec, spec],
        out_specs=pl.BlockSpec((seq_len, step * head_dim), lambda i: (0, i)),
        cost_estimate=pl.CostEstimate(flops=4 * heads * seq_len * seq_len * head_dim, bytes_accessed=8 * heads * seq_len * head_dim, transcendentals=heads * seq_len * seq_len),
        name="attention_core",
    )(q, k, v)


def attention_block(seq, attn_norm, w_query, w_key, w_value, w_out):
    normed = rms_norm(seq, attn_norm)
    q, k, v = (jnp.einsum('sd,dhc->hsc', normed, w, preferred_element_type=F32).astype(BF16) for w in (w_query, w_key, w_value))
    context = attention_core(q, k, v)
    w_flat = w_out.reshape(-1, w_out.shape[-1])
    proj_out = jnp.dot(context, w_flat, preferred_element_type=F32)
    return (seq.astype(F32) + proj_out).astype(BF16)


def pick_kernel(slot_ref, rows_ref, out_ref):
    exp_local, _, cap, _ = out_ref.shape
    toks = rows_ref.shape[1]
    want = lax.broadcasted_iota(jnp.int32, (cap, toks), 0)
    for e in range(exp_local):
        sel = (want == slot_ref[0, e:e + 1, :]).astype(F32).astype(BF16)
        out_ref[e, 0] = jnp.dot(sel, rows_ref[0], preferred_element_type=F32).astype(BF16)


def pick_rows(slots, rows, cap):
    srcs, exps, toks = slots.shape
    dim = rows.shape[-1]
    return pl.pallas_call(
        pick_kernel,
        grid=(srcs,),
        out_shape=jax.ShapeDtypeStruct((exps, srcs, cap, dim), BF16),
        in_specs=[pl.BlockSpec((1, exps, toks), lambda s: (s, 0, 0)), pl.BlockSpec((1, toks, dim), lambda s: (s, 0, 0))],
        out_specs=pl.BlockSpec((exps, 1, cap, dim), lambda s: (0, s, 0, 0)),
        cost_estimate=pl.CostEstimate(flops=2 * srcs * exps * cap * toks * dim, bytes_accessed=2 * srcs * (toks + exps * cap) * dim, transcendentals=0),
        name="pick_rows",
    )(slots, rows)


def ffn_kernel(x_ref, wg_ref, wu_ref, wd_ref, o_ref):
    _, srcs, cap, dim = x_ref.shape
    x = x_ref[0].reshape(srcs * cap, dim)
    gate_h = jnp.dot(x, wg_ref[0], preferred_element_type=F32)
    up_h = jnp.dot(x, wu_ref[0], preferred_element_type=F32)
    act = (jax.nn.silu(gate_h) * up_h).astype(BF16)
    y = jnp.dot(act, wd_ref[0], preferred_element_type=F32).astype(BF16)
    o_ref[:, 0] = y.reshape(srcs, cap, dim)


def expert_ffn(x, w_gate, w_up, w_down):
    exps, srcs, cap, dim = x.shape
    ff = w_gate.shape[-1]
    step = 8
    return pl.pallas_call(
        ffn_kernel,
        grid=(exps, srcs // step),
        out_shape=jax.ShapeDtypeStruct((srcs, exps, cap, dim), BF16),
        in_specs=[
            pl.BlockSpec((1, step, cap, dim), lambda e, s: (e, s, 0, 0)),
            pl.BlockSpec((1, dim, ff), lambda e, s: (e, 0, 0)),
            pl.BlockSpec((1, dim, ff), lambda e, s: (e, 0, 0)),
            pl.BlockSpec((1, ff, dim), lambda e, s: (e, 0, 0)),
        ],
        out_specs=pl.BlockSpec((step, 1, cap, dim), lambda e, s: (s, e, 0, 0)),
        cost_estimate=pl.CostEstimate(flops=6 * exps * srcs * cap * dim * ff, bytes_accessed=4 * exps * srcs * cap * dim + 6 * exps * dim * ff, transcendentals=exps * srcs * cap * ff),
        compiler_params=pltpu.CompilerParams(vmem_limit_bytes=VMEM_MAX),
        name="expert_ffn",
    )(x, w_gate, w_up, w_down)


def split3(x):
    hi = x.astype(BF16)
    rest = x - hi.astype(F32)
    mid = rest.astype(BF16)
    low = (rest - mid.astype(F32)).astype(BF16)
    return hi, mid, low


def ranks_of(mask, axis):
    toks = mask.shape[axis]
    row = lax.broadcasted_iota(jnp.int32, (toks, toks), 0)
    col = lax.broadcasted_iota(jnp.int32, (toks, toks), 1)
    if axis == mask.ndim - 1:
        tri = (row < col).astype(BF16)
        return jnp.dot(mask.astype(BF16), tri, preferred_element_type=F32).astype(jnp.int32)
    tri = (row > col).astype(BF16)
    return jnp.dot(tri, mask.astype(BF16), preferred_element_type=F32).astype(jnp.int32)


def slots_here(ids_all, first_exp, exp_local):
    mine = first_exp + jnp.arange(exp_local, dtype=jnp.int32)
    mask = jnp.any(ids_all[:, None] == mine[None, :, None, None], axis=2)
    srcs, exps, toks = mask.shape
    rank = ranks_of(mask.reshape(srcs * exps, toks), 1).reshape(srcs, exps, toks)
    return jnp.where(mask, rank, -1)


def home_select(ids, gates, num_exp, cap):
    hit = ids[:, :, None] == jnp.arange(num_exp, dtype=jnp.int32)[None, None, :]
    mask = jnp.any(hit, axis=1)
    gate = jnp.sum(jnp.where(hit, gates[:, :, None], 0.0), axis=1)
    rank = jnp.where(mask, ranks_of(mask, 0), -1)
    here = rank[:, :, None] == jnp.arange(cap, dtype=jnp.int32)[None, None, :]
    parts = [jnp.where(here, g.astype(F32)[:, :, None], 0.0).astype(BF16).reshape(ids.shape[0], num_exp * cap) for g in split3(gate)]
    return jnp.concatenate(parts, axis=0)


def solution(mesh):
    ep_size = mesh.shape['ep']
    sub_size = mesh.shape['sub']
    axes = ('ep', 'sub')
    tok_spec = P(('dp', 'ep', 'sub'), None, None)
    route_spec = P(None, ('dp', 'ep', 'sub'), None)
    exp_spec = P(('ep', 'sub'), None, None)

    def device_body(input_a, input_b, route_idx, route_gate, attn_norm, w_query, w_key, w_value, w_out, moe_norm, w_gate, w_up, w_down):
        exp_local = w_gate.shape[0]
        num_dev = ep_size * sub_size
        num_exp = exp_local * num_dev
        tok_count, top_k = route_idx.shape[1:]
        model_dim = input_a.shape[-1]
        cap = 3 * top_k * tok_count // (2 * num_exp)
        first_exp = lax.axis_index(axes) * exp_local

        ids_all = lax.all_gather(jnp.swapaxes(route_idx, 1, 2), axes, axis=0)

        hiddens, gathered = [], []
        for tokens in (input_a, input_b):
            hidden = attention_block(tokens.reshape(tok_count, model_dim), attn_norm, w_query, w_key, w_value, w_out)
            normed = rms_norm(hidden, moe_norm)
            gathered.append(lax.all_gather(normed, axes, axis=0))
            hiddens.append(hidden)

        outs = []
        for mb, tokens in enumerate((input_a, input_b)):
            slots = slots_here(ids_all[:, mb], first_exp, exp_local)
            picked = pick_rows(slots, gathered[mb], cap)
            expert_out = expert_ffn(picked, w_gate, w_up, w_down)
            returned = lax.all_to_all(expert_out, axes, 0, 0, tiled=True).reshape(num_exp * cap, model_dim)
            select = home_select(route_idx[mb], route_gate[mb], num_exp, cap)
            sums = jnp.dot(select, returned, preferred_element_type=F32).reshape(3, tok_count, model_dim)
            moe_sum = sums[0] + (sums[1] + sums[2])
            outs.append((hiddens[mb].astype(F32) + moe_sum).astype(BF16).reshape(tokens.shape))
        return outs[0], outs[1]

    return jax.shard_map(device_body, mesh=mesh, in_specs=(tok_spec, tok_spec, route_spec, route_spec, P(), P(), P(), P(), P(), P(), exp_spec, exp_spec, exp_spec), out_specs=(tok_spec, tok_spec), check_vma=False)
```

time: 2740 us -> 1400 us (0.51)
  the two profiles are of different devices: /device:TPU:97 before, /device:TPU:126 now
where the time goes in v1:
time: 1400 us; the launch traced here: 1390 us
  waiting for transfers between devices  792 us (57%)
  Pallas kernels  317 us (23%)
  matrix products  209 us (15%)
  other arithmetic  40.7 us (3%)
  starting transfers between devices  17.5 us (1%)
  between operations  14.3 us (1%)
    all_gather x2, waiting for transfers between devices, device_body(): gathered.append(lax.all_gather(normed, axes, axis=0))  513 us
    all_to_all x2, waiting for transfers between devices, device_body(): lax.all_to_all(expert_out, axes, 0, 0, tiled=True)  278 us
    pallas_call x2, Pallas kernels, expert_ffn(): pl.pallas_call(ffn_kernel, grid=(exps, srcs // step), out_shape=jax.Shape...  140 us
    pallas_call x2, Pallas kernels, pick_rows(): pl.pallas_call(pick_kernel, grid=(srcs,), out_shape=jax.ShapeDtypeStruct(...  117 us
    dot_general x2, matrix products, device_body(): jnp.dot(select, returned, preferred_element_type=F32)  94 us
    dot_general x6, matrix products, attention_block(): jnp.einsum('sd,dhc->hsc', normed, w, preferred_element_type=F32)  85.1 us
    pallas_call x2, Pallas kernels, attention_core(): pl.pallas_call(functools.partial(attn_kernel, head_dim ** (-0.5)), grid=(...  60.1 us
    dot_general x2, matrix products, attention_block(): proj_out = jnp.dot(context, w_flat, preferred_element_type=F32)  28.7 us
  transfers between devices with their start and end apart: 5, of which 3 were waited for; matrix products, arithmetic and copies ran while one was open for 15% of the time, Pallas kernels for 23%

profile of v1, /device:TPU:126, one launch (start us, length us, event | category | flops | bytes accessed | tf_op | source)
XLA Modules:
  0.0 1393.5 jit_solution(49056943379304936)
XLA Ops:
  7.2 0.1 all-gather.7.cloned.1.call-start
  7.2 0.7 all-gather.7.cloned.1.call-update
  8.0 0.1 all-gather.11.cloned.1.call-start
  8.0 2.1 fusion.42
  10.1 14.7 %convert_bitcast_fusion.v_ref = bf16[32,512,128]{2,1,0:T(8,128)(2,1)} fusion(bf16[2048,32,128]{2,1,0:T(8,128)(2,1)} %param.20, bf16[1,512,2048]{2,1,0:T(8,128)(2,1)} %param.14, f32[512]{0:T(512)S(1)} %add_rsqrt_fusion.1, f32[2048]{0:T(1024)} %param.17), kind=kOutput, calls=%fused_computation.70 | convolution fusion | flops 8596226048 | bytes 23078912 | tf_op jit(solution)/shard_map/sd,dhc->hsc/dot_general | solution.py:57
  24.8 14.1 %convert_bitcast_fusion.1.k_ref = bf16[32,512,128]{2,1,0:T(8,128)(2,1)} fusion(bf16[2048,32,128]{2,1,0:T(8,128)(2,1)} %param.19, bf16[1,512,2048]{2,1,0:T(8,128)(2,1)S(1)} %copy-done.4, f32[512]{0:T(512)S(1)} %add_rsqrt_fusion.1, f32[2048]{0:T(1024)S(1)} %copy-done.9), kind=kOutput, calls=%fused_computation.71 | convolution fusion | flops 8596226048 | bytes 23078912 | tf_op jit(solution)/shard_map/sd,dhc->hsc/dot_general | solution.py:57
  38.9 0.5 fusion.38
  39.4 14.2 %convert_bitcast_fusion.3.v_ref = bf16[32,512,128]{2,1,0:T(8,128)(2,1)} fusion(bf16[2048,32,128]{2,1,0:T(8,128)(2,1)} %param.20, bf16[1,512,2048]{2,1,0:T(8,128)(2,1)S(1)} %copy-done.5, f32[2048]{0:T(1024)S(1)} %copy-done.9, f32[512]{0:T(512)S(1)} %add_rsqrt_fusion.3), kind=kOutput, calls=%fused_computation.73 | convolution fusion | flops 8596226048 | bytes 23078912 | tf_op jit(solution)/shard_map/sd,dhc->hsc/dot_general | solution.py:57
  53.6 13.9 %convert_bitcast_fusion.4.k_ref = bf16[32,512,128]{2,1,0:T(8,128)(2,1)} fusion(bf16[2048,32,128]{2,1,0:T(8,128)(2,1)} %param.19, bf16[1,512,2048]{2,1,0:T(8,128)(2,1)S(1)} %copy-done.5, f32[2048]{0:T(1024)S(1)} %copy-done.9, f32[512]{0:T(512)S(1)} %add_rsqrt_fusion.3), kind=kOutput, calls=%fused_computation.74 | convolution fusion | flops 8596226048 | bytes 23078912 | tf_op jit(solution)/shard_map/sd,dhc->hsc/dot_general | solution.py:57
  67.6 14.2 %convert_bitcast_fusion.2.q_ref = bf16[32,512,128]{2,1,0:T(8,128)(2,1)} fusion(bf16[2048,32,128]{2,1,0:T(8,128)(2,1)} %param.18, bf16[1,512,2048]{2,1,0:T(8,128)(2,1)S(1)} %copy-done.4, f32[512]{0:T(512)S(1)} %add_rsqrt_fusion.1, f32[2048]{0:T(1024)S(1)} %copy-done.9), kind=kOutput, calls=%fused_computation.72 | convolution fusion | flops 8596226048 | bytes 23078912 | tf_op jit(solution)/shard_map/sd,dhc->hsc/dot_general | solution.py:57
  81.8 14.0 %convert_bitcast_fusion.5.q_ref = bf16[32,512,128]{2,1,0:T(8,128)(2,1)} fusion(bf16[2048,32,128]{2,1,0:T(8,128)(2,1)} %param.18, bf16[1,512,2048]{2,1,0:T(8,128)(2,1)S(1)} %copy-done.5, f32[2048]{0:T(1024)S(1)} %copy-done.9, f32[512]{0:T(512)S(1)} %add_rsqrt_fusion.3), kind=kOutput, calls=%fused_computation.75 | convolution fusion | flops 8596226048 | bytes 23078912 | tf_op jit(solution)/shard_map/sd,dhc->hsc/dot_general | solution.py:57
  95.7 29.7 %attention_core.3 = bf16[512,4096]{1,0:T(8,128)(2,1)} custom-call(bf16[32,512,128]{2,1,0:T(8,128)(2,1)} %convert_bitcast_fusion.2.q_ref, bf16[32,512,128]{2,1,0:T(8,128)(2,1)} %convert_bitcast_fusion.1.k_ref, bf16[32,512,128]{2,1,0:T(8,128)(2,1)} %convert_bitcast_fusion.v_ref), custom_call_target="tpu_custom_call" | custom-call | flops 4294967296 | bytes 16777216 | tf_op jit(solution)/shard_map/attention_core/pallas_call | solution.py:44
  125.4 14.5 %fusion.34 = (f32[512]{0:T(512)S(1)}, bf16[512,2048]{1,0:T(8,128)(2,1)S(1)}) fusion(bf16[512,4096]{1,0:T(8,128)(2,1)} %attention_core.3, bf16[4096,2048]{1,0:T(8,128)(2,1)} %bitcast.114, bf16[1,512,2048]{2,1,0:T(8,128)(2,1)} %param.14), kind=kOutput, calls=%fused_computation.54 | convolution fusion | flops 8596226048 | bytes 25167872 | tf_op jit(solution)/shard_map/dot_general | solution.py:60
  139.9 30.4 %attention_core.2 = bf16[512,4096]{1,0:T(8,128)(2,1)} custom-call(bf16[32,512,128]{2,1,0:T(8,128)(2,1)} %convert_bitcast_fusion.5.q_ref, bf16[32,512,128]{2,1,0:T(8,128)(2,1)} %convert_bitcast_fusion.4.k_ref, bf16[32,512,128]{2,1,0:T(8,128)(2,1)} %convert_bitcast_fusion.3.v_ref), custom_call_target="tpu_custom_call" | custom-call | flops 4294967296 | bytes 16777216 | tf_op jit(solution)/shard_map/attention_core/pallas_call | solution.py:44
  170.3 14.1 %fusion.30 = (f32[512]{0:T(512)S(1)}, bf16[512,2048]{1,0:T(8,128)(2,1)S(1)}) fusion(bf16[512,4096]{1,0:T(8,128)(2,1)} %attention_core.2, bf16[4096,2048]{1,0:T(8,128)(2,1)} %bitcast.115, bf16[1,512,2048]{2,1,0:T(8,128)(2,1)} %param.13), kind=kOutput, calls=%fused_computation.50 | convolution fusion | flops 8596226048 | bytes 25167872 | tf_op jit(solution)/shard_map/dot_general | solution.py:60
  184.5 3.1 fusion.36
  187.6 0.1 all-gather.11.cloned.1.call-update
  187.7 0.2 all-gather.9.cloned.1.call-start
  187.9 0.5 all-gather.9.cloned.1.call-update
  188.5 1.3 slice_bitcast_fusion.1
  189.8 1.9 compare_reduce_fusion
  191.7 0.1 reshape.153
  191.7 0.2 convolution_convert_fusion
  192.0 0.1 reshape.154
  192.1 0.8 broadcast_select_fusion.slot_ref
  192.9 189.6 %all-gather.11.cloned.1.call-done = bf16[16384,2048]{1,0:T(8,128)(2,1)} async-done(((bf16[512,2048]{1,0:T(8,128)(2,1)}), bf16[16384,2048]{1,0:T(8,128)(2,1)}) %all-gather.11.cloned.1.call-update) | async-done | bytes 67108880 | tf_op jit(solution)/shard_map/all_gather | solution.py:178
  382.5 58.3 %pick_rows.3.x_ref = bf16[4,32,48,2048]{3,2,1,0:T(8,128)(2,1)} custom-call(s32[32,4,512]{2,1,0:T(4,128)} %broadcast_select_fusion.slot_ref, bf16[32,512,2048]{2,1,0:T(8,128)(2,1)} %bitcast.32.rows_ref), custom_call_target="tpu_custom_call" | custom-call | flops 12884901888 | bytes 92274688 | tf_op jit(solution)/shard_map/pick_rows/pallas_call | solution.py:76
  440.8 69.9 %expert_ffn.3 = bf16[32,4,48,2048]{3,2,1,0:T(8,128)(2,1)} custom-call(bf16[4,32,48,2048]{3,2,1,0:T(8,128)(2,1)} %pick_rows.3.x_ref, bf16[4,2048,768]{2,1,0:T(8,128)(2,1)} %wg_ref.3, bf16[4,2048,768]{2,1,0:T(8,128)(2,1)} %wu_ref.3, bf16[4,768,2048]{2,1,0:T(8,128)(2,1)} %wd_ref.3), custom_call_target="tpu_custom_call" | custom-call | flops 57982058496 | bytes 88080384 | tf_op jit(solution)/shard_map/expert_ffn/pallas_call | solution.py:101
  510.7 6.9 all-to-all-start.1
  517.7 0.1 reshape.149
  517.7 0.2 convolution_convert_fusion.2
  518.0 0.1 reshape.150
  518.1 0.8 broadcast_select_fusion.1.slot_ref
  518.9 323.6 %all-gather.9.cloned.1.call-done = bf16[16384,2048]{1,0:T(8,128)(2,1)} async-done(((bf16[512,2048]{1,0:T(8,128)(2,1)}), bf16[16384,2048]{1,0:T(8,128)(2,1)}) %all-gather.9.cloned.1.call-update) | async-done | bytes 67108880 | tf_op jit(solution)/shard_map/all_gather | solution.py:178
  842.5 58.3 %pick_rows.2.x_ref = bf16[4,32,48,2048]{3,2,1,0:T(8,128)(2,1)} custom-call(s32[32,4,512]{2,1,0:T(4,128)} %broadcast_select_fusion.1.slot_ref, bf16[32,512,2048]{2,1,0:T(8,128)(2,1)} %bitcast.16.rows_ref), custom_call_target="tpu_custom_call" | custom-call | flops 12884901888 | bytes 92274688 | tf_op jit(solution)/shard_map/pick_rows/pallas_call | solution.py:76
  900.8 69.9 %expert_ffn.2 = bf16[32,4,48,2048]{3,2,1,0:T(8,128)(2,1)} custom-call(bf16[4,32,48,2048]{3,2,1,0:T(8,128)(2,1)} %pick_rows.2.x_ref, bf16[4,2048,768]{2,1,0:T(8,128)(2,1)} %wg_ref.3, bf16[4,2048,768]{2,1,0:T(8,128)(2,1)} %wu_ref.3, bf16[4,768,2048]{2,1,0:T(8,128)(2,1)} %wd_ref.3), custom_call_target="tpu_custom_call" | custom-call | flops 57982058496 | bytes 88080384 | tf_op jit(solution)/shard_map/expert_ffn/pallas_call | solution.py:101
  970.8 10.3 all-to-all-start
  981.1 0.1 copy.40
  981.2 0.1 copy.42
  981.3 2.5 select_reduce_fusion.1
  983.8 0.1 fusion.81
  983.9 0.1 copy.43
  984.0 0.1 copy.44
  984.2 0.1 copy.45
  984.3 0.1 copy.49
  984.4 0.1 copy.51
  984.5 2.5 select_reduce_fusion
  987.0 0.1 fusion.80
  987.1 0.1 copy.52
  987.2 0.1 copy.53
  987.3 0.1 copy.54
  987.5 2.9 fusion.65
  990.4 0.3 fusion.67
  990.7 0.1 copy.41
  990.8 2.9 fusion.64
  993.7 0.3 fusion.66
  994.1 0.1 copy.50
  994.2 0.1 eq.109
  994.3 14.6 %fusion.26 = (bf16[512,6144]{0,1:T(8,128)(2,1)}, bf16[512,6144]{0,1:T(8,128)(2,1)}, bf16[512,6144]{0,1:T(8,128)(2,1)}, bf16[512,6144]{0,1:T(8,128)(2,1)}, bf16[5...) fusion(bf16[512,128]{0,1:T(8,128)(2,1)S(1)} %copy.52, s32[512,128]{0,1:T(8,128)S(1)} %copy.50, s32[6144]{0:T(1024)S(1)} %eq.109, ...), kind=kLoop, calls=%fused_computation.29 | loop fusion | flops 25165824 | bytes 39084032 | tf_op jit(solution)/shard_map/convert_element_type | solution.py:151
  1008.9 46.9 %fusion.6 = f32[1536,2048]{1,0:T(8,128)S(1)} fusion(bf16[6144,2048]{1,0:T(8,128)(2,1)} %bitcast.33, bf16[512,6144]{0,1:T(8,128)(2,1)} %get-tuple-element.7, bf16[512,6144]{0,1:T(8,128)(2,1)} %get-tuple-element.8, bf16[512,6144]{0,1:T(8,128)(2,1)} %get-tuple-element.6), kind=kOutput, calls=%fused_computation.6 | convolution fusion | flops 38711328768 | bytes 56623104 | tf_op jit(solution)/shard_map/dot_general | solution.py:188
  1055.8 3.0 fusion.62
  1058.8 277.9 %all-to-all-done = bf16[32,4,48,2048]{3,2,1,0:T(8,128)(2,1)} async-done(((bf16[32,4,48,2048]{3,2,1,0:T(8,128)(2,1)}), bf16[32,4,48,2048]{3,2,1,0:T(8,128)(2,1)}, u32[]{:S(2)}, u32[]{:S(2)}) %all-to-all-start) | async-done | bytes 25165856 | tf_op jit(solution)/shard_map/all_to_all | solution.py:186
  1336.7 47.1 %fusion = f32[1536,2048]{1,0:T(8,128)S(1)} fusion(bf16[6144,2048]{1,0:T(8,128)(2,1)} %bitcast.17, bf16[512,6144]{0,1:T(8,128)(2,1)} %get-tuple-element.23, bf16[512,6144]{0,1:T(8,128)(2,1)} %get-tuple-element.22, bf16[512,6144]{0,1:T(8,128)(2,1)} %get-tuple-element.24), kind=kOutput, calls=%fused_computation | convolution fusion | flops 38711328768 | bytes 56623104 | tf_op jit(solution)/shard_map/dot_general | solution.py:188
  1383.8 3.0 fusion.63
  (29 shorter events, 0.1 us)
Async XLA Ops:
  7.2 181.3 %all-gather.7.cloned.1.call-start = ((), (), s32[]{:S(2)}) async-start(), calls=%async_computation.2 | async-start | bytes 1081344 | tf_op jit(solution)/shard_map/all_gather | solution.py:172
  8.0 374.5 %all-gather.11.cloned.1.call-start = ((), (), s32[]{:S(2)}) async-start(), calls=%async_computation.4 | async-start | bytes 69206016 | tf_op jit(solution)/shard_map/all_gather | solution.py:178
  10.1 14.7 %copy-start.4 = (bf16[1,512,2048]{2,1,0:T(8,128)(2,1)S(1)}, bf16[1,512,2048]{2,1,0:T(8,128)(2,1)}, u32[]{:S(2)}) copy-start(bf16[1,512,2048]{2,1,0:T(8,128)(2,1)} %param.14) | copy-start | bytes 6291460
  10.1 14.7 %copy-start.9 = (f32[2048]{0:T(1024)S(1)}, f32[2048]{0:T(1024)}, u32[]{:S(2)}) copy-start(f32[2048]{0:T(1024)} %param.17) | copy-start | bytes 24580
  24.8 14.1 %copy-start.5 = (bf16[1,512,2048]{2,1,0:T(8,128)(2,1)S(1)}, bf16[1,512,2048]{2,1,0:T(8,128)(2,1)}, u32[]{:S(2)}) copy-start(bf16[1,512,2048]{2,1,0:T(8,128)(2,1)} %param.13) | copy-start | bytes 6291460
  139.9 44.6 %copy-start.2 = (bf16[512,2048]{1,0:T(8,128)(2,1)}, bf16[512,2048]{1,0:T(8,128)(2,1)S(1)}, u32[]{:S(2)}) copy-start(bf16[512,2048]{1,0:T(8,128)(2,1)S(1)} %get-tuple-element.28) | copy-start | bytes 6291460
  170.3 14.2 %copy-start.8 = (f32[2048]{0:T(1024)S(1)}, f32[2048]{0:T(1024)}, u32[]{:S(2)}) copy-start(f32[2048]{0:T(1024)} %param.22) | copy-start | bytes 24580
  184.5 3.1 copy-start
  187.7 654.8 %all-gather.9.cloned.1.call-start = ((), (), s32[]{:S(2)}) async-start(), calls=%async_computation.3 | async-start | bytes 69206016 | tf_op jit(solution)/shard_map/all_gather | solution.py:178
  510.7 460.0 %all-to-all-start.1 = ((bf16[32,4,48,2048]{3,2,1,0:T(8,128)(2,1)}), bf16[32,4,48,2048]{3,2,1,0:T(8,128)(2,1)}, u32[]{:S(2)}, u32[]{:S(2)}) async-start(bf16[32,4,48,2048]{3,2,1,0:T(8,128)(2,1)} %expert_ffn.3), calls=%async_computation.1 | async-start | bytes 50331648 | tf_op jit(solution)/shard_map/all_to_all | solution.py:186
  970.8 10.3 copy-start.6
  970.8 10.4 copy-start.7
  970.8 365.9 %all-to-all-start = ((bf16[32,4,48,2048]{3,2,1,0:T(8,128)(2,1)}), bf16[32,4,48,2048]{3,2,1,0:T(8,128)(2,1)}, u32[]{:S(2)}, u32[]{:S(2)}) async-start(bf16[32,4,48,2048]{3,2,1,0:T(8,128)(2,1)} %expert_ffn.2), calls=%async_computation | async-start | bytes 50331648 | tf_op jit(solution)/shard_map/all_to_all | solution.py:186
  1008.9 46.9 %copy-start.3 = (bf16[512,2048]{1,0:T(8,128)(2,1)S(1)}, bf16[512,2048]{1,0:T(8,128)(2,1)}, u32[]{:S(2)}) copy-start(bf16[512,2048]{1,0:T(8,128)(2,1)} %copy-done.2) | copy-start | bytes 6291460
  1336.7 47.1 %copy-start.1 = (bf16[512,2048]{1,0:T(8,128)(2,1)S(1)}, bf16[512,2048]{1,0:T(8,128)(2,1)}, u32[]{:S(2)}) copy-start(bf16[512,2048]{1,0:T(8,128)(2,1)} %copy-done) | copy-start | bytes 6291460
Sparse Core Ops, SparseCore 0:
  10.1 35.9 all-gather.6
  187.8 194.6 all-gather.10
  385.2 457.2 all-gather.8

commit v2 on v1

v2 whole, which is shorter than its diff:
```python
import functools

import jax
import jax.numpy as jnp
from jax import lax
from jax.experimental import pallas as pl
from jax.experimental.pallas import tpu as pltpu
from jax.sharding import PartitionSpec as P

NORM_EPS = 1e-6
VMEM_MAX = 60 * 1024 * 1024
F32 = jnp.float32
BF16 = jnp.bfloat16


def rms_norm(values, norm_gain):
    acc_f32 = values.astype(F32)
    inv_rms = lax.rsqrt(jnp.mean(acc_f32 * acc_f32, axis=-1, keepdims=True) + NORM_EPS)
    return (acc_f32 * inv_rms * norm_gain).astype(BF16)


def attn_kernel(scale, first, q_ref, *refs):
    k_refs, v_refs, o_ref = refs[:first + 1], refs[first + 1:2 * first + 2], refs[-1]
    heads, q_len, head_dim = q_ref.shape
    parts = 2 if first == 0 and q_len >= 512 else 1
    rows_per = q_len // parts
    for h in range(heads):
        for part in range(parts):
            q = q_ref[h, part * rows_per:(part + 1) * rows_per, :]
            spans = [(k_refs[i], v_refs[i], 0, k_refs[i].shape[1], False) for i in range(first)]
            if part:
                spans.append((k_refs[first], v_refs[first], 0, part * rows_per, False))
            spans.append((k_refs[first], v_refs[first], part * rows_per, (part + 1) * rows_per, True))
            scores = []
            for k_ref, _, lo, hi, diagonal in spans:
                s = lax.dot_general(q, k_ref[h, lo:hi, :], (((1,), (1,)), ((), ())), preferred_element_type=F32) * scale
                if diagonal:
                    rows = lax.broadcasted_iota(jnp.int32, s.shape, 0)
                    cols = lax.broadcasted_iota(jnp.int32, s.shape, 1)
                    s = jnp.where(rows >= cols, s, -jnp.inf)
                scores.append(s)
            top = functools.reduce(jnp.maximum, [jnp.max(s, axis=-1, keepdims=True) for s in scores])
            probs = [jnp.exp(s - top) for s in scores]
            inv = 1.0 / functools.reduce(jnp.add, [jnp.sum(p, axis=-1, keepdims=True) for p in probs])
            o = None
            for p, (_, v_ref, lo, hi, _) in zip(probs, spans):
                term = jnp.dot((p * inv).astype(BF16), v_ref[h, lo:hi, :], preferred_element_type=F32)
                o = term if o is None else o + term
            o_ref[part * rows_per:(part + 1) * rows_per, h * head_dim:(h + 1) * head_dim] = o.astype(BF16)


def attention_core(q, ks, vs):
    heads, q_len, head_dim = q.shape
    step = 4
    spec = lambda t: pl.BlockSpec((step, t.shape[1], head_dim), lambda i: (i, 0, 0))
    keys = sum(k.shape[1] for k in ks)
    return pl.pallas_call(
        functools.partial(attn_kernel, head_dim ** -0.5, len(ks) - 1),
        grid=(heads // step,),
        out_shape=jax.ShapeDtypeStruct((q_len, heads * head_dim), BF16),
        in_specs=[spec(t) for t in (q, *ks, *vs)],
        out_specs=pl.BlockSpec((q_len, step * head_dim), lambda i: (0, i)),
        cost_estimate=pl.CostEstimate(flops=4 * heads * q_len * keys * head_dim, bytes_accessed=4 * heads * (q_len + keys) * head_dim, transcendentals=heads * q_len * keys),
        name="attention_core",
    )(q, *ks, *vs)


def attention_rows(rows, ks, vs, attn_norm, w_query, w_key, w_value, w_out):
    normed = rms_norm(rows, attn_norm)
    q, k, v = (jnp.einsum('sd,dhc->hsc', normed, w, preferred_element_type=F32).astype(BF16) for w in (w_query, w_key, w_value))
    ks, vs = ks + [k], vs + [v]
    context = attention_core(q, ks, vs)
    proj_out = jnp.dot(context, w_out.reshape(-1, w_out.shape[-1]), preferred_element_type=F32)
    return (rows.astype(F32) + proj_out).astype(BF16), ks, vs


def pick_kernel(slot_ref, *refs):
    row_refs, out_ref = refs[:-1], refs[-1]
    exp_local, _, cap, dim = out_ref.shape
    total = None
    lo = 0
    for rows_ref in row_refs:
        toks = rows_ref.shape[1]
        want = lax.broadcasted_iota(jnp.int32, (cap, toks), 0)
        sel = jnp.concatenate([(want == slot_ref[0, e:e + 1, lo:lo + toks]).astype(F32) for e in range(exp_local)], axis=0).astype(BF16)
        term = jnp.dot(sel, rows_ref[0], preferred_element_type=F32)
        total = term if total is None else total + term
        lo += toks
    out_ref[:, 0] = total.astype(BF16).reshape(exp_local, cap, dim)


def pick_rows(slots, ranges, cap):
    srcs, exps, toks = slots.shape
    dim = ranges[0].shape[-1]
    return pl.pallas_call(
        pick_kernel,
        grid=(srcs,),
        out_shape=jax.ShapeDtypeStruct((exps, srcs, cap, dim), BF16),
        in_specs=[pl.BlockSpec((1, exps, toks), lambda s: (s, 0, 0))] + [pl.BlockSpec((1, r.shape[1], dim), lambda s: (s, 0, 0)) for r in ranges],
        out_specs=pl.BlockSpec((exps, 1, cap, dim), lambda s: (0, s, 0, 0)),
        cost_estimate=pl.CostEstimate(flops=2 * srcs * exps * cap * toks * dim, bytes_accessed=2 * srcs * (toks + exps * cap) * dim, transcendentals=0),
        name="pick_rows",
    )(slots, *ranges)


def ffn_kernel(x_ref, wg_ref, wu_ref, wd_ref, *o_refs):
    _, srcs, cap, dim = x_ref.shape
    x = x_ref[0].reshape(srcs * cap, dim)
    gate_h = jnp.dot(x, wg_ref[0], preferred_element_type=F32)
    up_h = jnp.dot(x, wu_ref[0], preferred_element_type=F32)
    act = (jax.nn.silu(gate_h) * up_h).astype(BF16)
    y = jnp.dot(act, wd_ref[0], preferred_element_type=F32).astype(BF16)
    lo = 0
    for o_ref in o_refs:
        width = o_ref.shape[-1]
        o_ref[:, 0] = y[:, lo:lo + width].reshape(srcs, cap, width)
        lo += width


def expert_ffn(x, w_gate, w_up, w_down, pieces):
    exps, srcs, cap, dim = x.shape
    ff = w_gate.shape[-1]
    step = 8
    width = dim // pieces
    return pl.pallas_call(
        ffn_kernel,
        grid=(exps, srcs // step),
        out_shape=[jax.ShapeDtypeStruct((srcs, exps, cap, width), BF16)] * pieces,
        in_specs=[
            pl.BlockSpec((1, step, cap, dim), lambda e, s: (e, s, 0, 0)),
            pl.BlockSpec((1, dim, ff), lambda e, s: (e, 0, 0)),
            pl.BlockSpec((1, dim, ff), lambda e, s: (e, 0, 0)),
            pl.BlockSpec((1, ff, dim), lambda e, s: (e, 0, 0)),
        ],
        out_specs=[pl.BlockSpec((step, 1, cap, width), lambda e, s: (s, e, 0, 0))] * pieces,
        cost_estimate=pl.CostEstimate(flops=6 * exps * srcs * cap * dim * ff, bytes_accessed=4 * exps * srcs * cap * dim + 6 * exps * dim * ff, transcendentals=exps * srcs * cap * ff),
        compiler_params=pltpu.CompilerParams(vmem_limit_bytes=VMEM_MAX),
        name="expert_ffn",
    )(x, w_gate, w_up, w_down)


def split3(x):
    hi = x.astype(BF16)
    rest = x - hi.astype(F32)
    mid = rest.astype(BF16)
    low = (rest - mid.astype(F32)).astype(BF16)
    return hi, mid, low


def ranks_of(mask, axis):
    toks = mask.shape[axis]
    row = lax.broadcasted_iota(jnp.int32, (toks, toks), 0)
    col = lax.broadcasted_iota(jnp.int32, (toks, toks), 1)
    if axis == mask.ndim - 1:
        tri = (row < col).astype(BF16)
        return jnp.dot(mask.astype(BF16), tri, preferred_element_type=F32).astype(jnp.int32)
    tri = (row > col).astype(BF16)
    return jnp.dot(tri, mask.astype(BF16), preferred_element_type=F32).astype(jnp.int32)


def slots_here(ids_all, first_exp, exp_local):
    mine = first_exp + jnp.arange(exp_local, dtype=jnp.int32)
    mask = jnp.any(ids_all[:, None] == mine[None, :, None, None], axis=2)
    srcs, exps, toks = mask.shape
    rank = ranks_of(mask.reshape(srcs * exps, toks), 1).reshape(srcs, exps, toks)
    return jnp.where(mask, rank, -1)


def home_select(ids, gates, num_exp, cap):
    hit = ids[:, :, None] == jnp.arange(num_exp, dtype=jnp.int32)[None, None, :]
    mask = jnp.any(hit, axis=1)
    gate = jnp.sum(jnp.where(hit, gates[:, :, None], 0.0), axis=1)
    rank = jnp.where(mask, ranks_of(mask, 0), -1)
    here = rank[:, :, None] == jnp.arange(cap, dtype=jnp.int32)[None, None, :]
    parts = [jnp.where(here, g.astype(F32)[:, :, None], 0.0).astype(BF16).reshape(ids.shape[0], num_exp * cap) for g in split3(gate)]
    return jnp.concatenate(parts, axis=0)


def solution(mesh):
    ep_size = mesh.shape['ep']
    sub_size = mesh.shape['sub']
    axes = ('ep', 'sub')
    tok_spec = P(('dp', 'ep', 'sub'), None, None)
    route_spec = P(None, ('dp', 'ep', 'sub'), None)
    exp_spec = P(('ep', 'sub'), None, None)

    def device_body(input_a, input_b, route_idx, route_gate, attn_norm, w_query, w_key, w_value, w_out, moe_norm, w_gate, w_up, w_down):
        exp_local = w_gate.shape[0]
        num_dev = ep_size * sub_size
        num_exp = exp_local * num_dev
        tok_count, top_k = route_idx.shape[1:]
        model_dim = input_a.shape[-1]
        cap = 3 * top_k * tok_count // (2 * num_exp)
        first_exp = lax.axis_index(axes) * exp_local

        ids_all = lax.all_gather(jnp.swapaxes(route_idx, 1, 2), axes, axis=0)

        weights = (attn_norm, w_query, w_key, w_value, w_out)
        hiddens, gathered = [], []
        after = None
        for tokens, ranges in ((input_a, 2), (input_b, 1)):
            rows_all = tokens.reshape(tok_count, model_dim)
            step = tok_count // ranges
            ks, vs, parts, blocks = [], [], [], []
            for r in range(ranges):
                rows = rows_all[r * step:(r + 1) * step]
                if after is not None:
                    rows, after = lax.optimization_barrier((rows, after))
                hidden, ks, vs = attention_rows(rows, ks, vs, *weights)
                after = rms_norm(hidden, moe_norm)
                blocks.append(lax.all_gather(after, axes, axis=0))
                parts.append(hidden)
            hiddens.append(jnp.concatenate(parts, axis=0) if ranges > 1 else parts[0])
            gathered.append(blocks)

        expert_outs = []
        for mb, pieces in ((0, 1), (1, 1)):
            slots = slots_here(ids_all[:, mb], first_exp, exp_local)
            picked = pick_rows(slots, gathered[mb], cap)
            expert_outs.append(expert_ffn(picked, w_gate, w_up, w_down, pieces))
            if mb == 0:
                expert_outs[0], gathered[1] = lax.optimization_barrier((expert_outs[0], gathered[1]))

        outs = []
        for mb, tokens in enumerate((input_a, input_b)):
            select = home_select(route_idx[mb], route_gate[mb], num_exp, cap)
            pieces = []
            lo = 0
            for piece in expert_outs[mb]:
                width = piece.shape[-1]
                returned = lax.all_to_all(piece, axes, 0, 0, tiled=True).reshape(num_exp * cap, width)
                sums = jnp.dot(select, returned, preferred_element_type=F32).reshape(3, tok_count, width)
                moe_sum = sums[0] + (sums[1] + sums[2])
                pieces.append((hiddens[mb][:, lo:lo + width].astype(F32) + moe_sum).astype(BF16))
                lo += width
            outs.append((jnp.concatenate(pieces, axis=1) if len(pieces) > 1 else pieces[0]).reshape(tokens.shape))
        return outs[0], outs[1]

    return jax.shard_map(device_body, mesh=mesh, in_specs=(tok_spec, tok_spec, route_spec, route_spec, P(), P(), P(), P(), P(), P(), exp_spec, exp_spec, exp_spec), out_specs=(tok_spec, tok_spec), check_vma=False)
```

time: 1400 us -> 1280 us (0.914)
  waiting for transfers between devices: 792 us -> 655 us
  matrix products: 209 us -> 251 us
  Pallas kernels: 317 us -> 287 us
    all_gather x2 -> x3, waiting for transfers between devices: 513 us -> 137 us  [device_body(): blocks.append(lax.all_gather(after, axes, axis=0))]
    all_to_all x2, waiting for transfers between devices: 278 us -> 517 us  [device_body(): lax.all_to_all(piece, axes, 0, 0, tiled=True).reshape(num_exp * cap, width)]
    dot_general x8 -> x12, matrix products: 114 us -> 156 us  [the longest x9 120 us: attention_rows(): jnp.einsum('sd,dhc->hsc', normed, w, preferred_element_type=F32)]
    pallas_call x2, Pallas kernels: 117 us -> 91 us  [pick_rows(): pl.pallas_call(pick_kernel, grid=(srcs,), out_shape=jax.ShapeDtypeStruct(...]
    pallas_call x4 -> x5, Pallas kernels: 200 us -> 196 us  [the longest x2 140 us: expert_ffn(): pl.pallas_call(ffn_kernel, grid=(exps, srcs // step), out_shape=[jax.Shap...]
  transfers between devices with their start and end apart: 5 -> 6, of which waited for: 3 -> 4; matrix products, arithmetic and copies ran while one was open for 15% -> 19% of each run, Pallas kernels for 23% -> 23%
where the time goes in v2:
time: 1280 us; the launch traced here: 1270 us
  waiting for transfers between devices  655 us (51%)
  Pallas kernels  287 us (22%)
  matrix products  251 us (20%)
  other arithmetic  41.6 us (3%)
  between operations  14.7 us (1%)
  starting transfers between devices  14.4 us (1%)
    all_to_all x2, waiting for transfers between devices, device_body(): lax.all_to_all(piece, axes, 0, 0, tiled=True).reshape(num_exp * cap, width)  517 us
    pallas_call x2, Pallas kernels, expert_ffn(): pl.pallas_call(ffn_kernel, grid=(exps, srcs // step), out_shape=[jax.Shap...  140 us
    all_gather x3, waiting for transfers between devices, device_body(): blocks.append(lax.all_gather(after, axes, axis=0))  137 us
    dot_general x9, matrix products, attention_rows(): jnp.einsum('sd,dhc->hsc', normed, w, preferred_element_type=F32)  120 us
    dot_general x2, matrix products, device_body(): jnp.dot(select, returned, preferred_element_type=F32)  93.8 us
    pallas_call x2, Pallas kernels, pick_rows(): pl.pallas_call(pick_kernel, grid=(srcs,), out_shape=jax.ShapeDtypeStruct(...  91 us
    pallas_call x3, Pallas kernels, attention_core(): pl.pallas_call(functools.partial(attn_kernel, head_dim ** (-0.5), len(ks)...  56 us
    dot_general x3, matrix products, attention_rows(): jnp.dot(context, w_out.reshape(-1, w_out.shape[-1]), preferred_element_ty...  36.1 us
  transfers between devices with their start and end apart: 6, of which 4 were waited for; matrix products, arithmetic and copies ran while one was open for 19% of the time, Pallas kernels for 23%

profile of v2, /device:TPU:126, one launch (start us, length us, event | category | flops | bytes accessed | tf_op | source)
XLA Modules:
  0.0 1270.0 jit_solution(15805687488813080578)
XLA Ops:
  7.2 0.7 all-gather.9.cloned.1.call-update
  8.0 1.5 fusion.65
  9.6 13.3 %convert_bitcast_fusion.7.refs_0_ = bf16[32,256,128]{2,1,0:T(8,128)(2,1)} fusion(bf16[2048,32,128]{2,1,0:T(8,128)(2,1)} %param.19, f32[2048]{0:T(1024)} %param.17, f32[256]{0:T(256)S(1)} %add_rsqrt_fusion.5, bf16[1,512,2048]{2,1,0:T(8,128)(2,1)} %param.13), kind=kOutput, calls=%fused_computation.104 | convolution fusion | flops 4298113024 | bytes 19932160 | tf_op jit(solution)/shard_map/sd,dhc->hsc/dot_general | solution.py:70
  22.8 12.9 %convert_bitcast_fusion.6.refs_1_.refs_2_ = bf16[32,256,128]{2,1,0:T(8,128)(2,1)} fusion(bf16[2048,32,128]{2,1,0:T(8,128)(2,1)} %param.20, f32[2048]{0:T(1024)S(1)} %copy-done.11, f32[256]{0:T(256)S(1)} %add_rsqrt_fusion.5, bf16[1,512,2048]{2,1,0:T(8,128)(2,1)S(1)} %copy-done.7), kind=kOutput, calls=%fused_computation.103 | convolution fusion | flops 4298113024 | bytes 19932160 | tf_op jit(solution)/shard_map/sd,dhc->hsc/dot_general | solution.py:70
  35.7 13.1 %convert_bitcast_fusion.8.q_ref = bf16[32,256,128]{2,1,0:T(8,128)(2,1)} fusion(bf16[2048,32,128]{2,1,0:T(8,128)(2,1)} %param.18, f32[2048]{0:T(1024)S(1)} %copy-done.11, f32[256]{0:T(256)S(1)} %add_rsqrt_fusion.5, bf16[1,512,2048]{2,1,0:T(8,128)(2,1)S(1)} %copy-done.7), kind=kOutput, calls=%fused_computation.105 | convolution fusion | flops 4298113024 | bytes 19932160 | tf_op jit(solution)/shard_map/sd,dhc->hsc/dot_general | solution.py:70
  48.8 11.1 attention_core.3
  59.9 11.1 fusion.56
  71.0 1.0 copy-done.2
  72.0 1.3 fusion.58
  73.4 0.5 all-gather.13.cloned.1.call-start
  73.9 0.3 fusion.62
  74.2 12.9 %convert_bitcast_fusion.4.refs_1_ = bf16[32,256,128]{2,1,0:T(8,128)(2,1)} fusion(bf16[2048,32,128]{2,1,0:T(8,128)(2,1)} %param.19, bf16[256,2048]{1,0:T(8,128)(2,1)S(1)} %slice_bitcast_fusion, f32[256]{0:T(256)S(1)} %add_rsqrt_fusion.3, f32[2048]{0:T(1024)S(1)} %copy-done.11), kind=kOutput, calls=%fused_computation.101 | convolution fusion | flops 4298113024 | bytes 19932160 | tf_op jit(solution)/shard_map/sd,dhc->hsc/dot_general | solution.py:70
  87.1 12.9 %convert_bitcast_fusion.3.refs_3_ = bf16[32,256,128]{2,1,0:T(8,128)(2,1)} fusion(bf16[2048,32,128]{2,1,0:T(8,128)(2,1)} %param.20, bf16[256,2048]{1,0:T(8,128)(2,1)S(1)} %slice_bitcast_fusion, f32[256]{0:T(256)S(1)} %add_rsqrt_fusion.3, f32[2048]{0:T(1024)S(1)} %copy-done.11), kind=kOutput, calls=%fused_computation.100 | convolution fusion | flops 4298113024 | bytes 19932160 | tf_op jit(solution)/shard_map/sd,dhc->hsc/dot_general | solution.py:70
  100.0 13.0 %convert_bitcast_fusion.5.q_ref = bf16[32,256,128]{2,1,0:T(8,128)(2,1)} fusion(bf16[2048,32,128]{2,1,0:T(8,128)(2,1)} %param.18, bf16[256,2048]{1,0:T(8,128)(2,1)S(1)} %slice_bitcast_fusion, f32[256]{0:T(256)S(1)} %add_rsqrt_fusion.3, f32[2048]{0:T(1024)S(1)} %copy-done.11), kind=kOutput, calls=%fused_computation.102 | convolution fusion | flops 4298113024 | bytes 19932160 | tf_op jit(solution)/shard_map/sd,dhc->hsc/dot_general | solution.py:70
  113.0 15.9 %attention_core.4 = bf16[256,4096]{1,0:T(8,128)(2,1)} custom-call(bf16[32,256,128]{2,1,0:T(8,128)(2,1)} %convert_bitcast_fusion.5.q_ref, bf16[32,256,128]{2,1,0:T(8,128)(2,1)} %convert_bitcast_fusion.7.refs_0_, bf16[32,256,128]{2,1,0:T(8,128)(2,1)} %convert_bitcast_fusion.4.refs_1_, bf16[32,256,128]{2,1,0:T(8,128)(2,1)} %convert_bitcast_fusion.6.refs_1_.refs_2_, ...), custom_call_target="tpu_custom_call" | custom-call | flops 2147483648 | bytes 12582912 | tf_op jit(solution)/shard_map/attention_core/pallas_call | solution.py:57
  128.9 11.0 fusion.59
  140.0 1.0 copy-done.4
  141.0 1.3 fusion.61
  142.3 0.3 all-gather.15.cloned.1.call-start
  142.6 0.5 fusion.36
  143.1 14.0 %convert_bitcast_fusion.1.refs_0_ = bf16[32,512,128]{2,1,0:T(8,128)(2,1)} fusion(bf16[2048,32,128]{2,1,0:T(8,128)(2,1)} %param.19, bf16[512,2048]{1,0:T(8,128)(2,1)S(1)} %bitcast.124, f32[2048]{0:T(1024)S(1)} %copy-done.11, f32[512]{0:T(512)S(1)} %add_rsqrt_fusion.1), kind=kOutput, calls=%fused_computation.65 | convolution fusion | flops 8596226048 | bytes 23078912 | tf_op jit(solution)/shard_map/sd,dhc->hsc/dot_general | solution.py:70
  157.1 13.9 %convert_bitcast_fusion.refs_1_ = bf16[32,512,128]{2,1,0:T(8,128)(2,1)} fusion(bf16[2048,32,128]{2,1,0:T(8,128)(2,1)} %param.20, bf16[512,2048]{1,0:T(8,128)(2,1)S(1)} %bitcast.125, f32[2048]{0:T(1024)S(1)} %copy-done.11, f32[512]{0:T(512)S(1)} %add_rsqrt_fusion.1), kind=kOutput, calls=%fused_computation.64 | convolution fusion | flops 8596226048 | bytes 23078912 | tf_op jit(solution)/shard_map/sd,dhc->hsc/dot_general | solution.py:70
  171.0 14.3 %convert_bitcast_fusion.2.q_ref = bf16[32,512,128]{2,1,0:T(8,128)(2,1)} fusion(bf16[2048,32,128]{2,1,0:T(8,128)(2,1)} %param.18, bf16[512,2048]{1,0:T(8,128)(2,1)S(1)} %bitcast.126, f32[2048]{0:T(1024)S(1)} %copy-done.11, f32[512]{0:T(512)S(1)} %add_rsqrt_fusion.1), kind=kOutput, calls=%fused_computation.66 | convolution fusion | flops 8596226048 | bytes 23078912 | tf_op jit(solution)/shard_map/sd,dhc->hsc/dot_general | solution.py:70
  185.3 29.0 %attention_core.5 = bf16[512,4096]{1,0:T(8,128)(2,1)} custom-call(bf16[32,512,128]{2,1,0:T(8,128)(2,1)} %convert_bitcast_fusion.2.q_ref, bf16[32,512,128]{2,1,0:T(8,128)(2,1)} %convert_bitcast_fusion.1.refs_0_, bf16[32,512,128]{2,1,0:T(8,128)(2,1)} %convert_bitcast_fusion.refs_1_), custom_call_target="tpu_custom_call" | custom-call | flops 4294967296 | bytes 16777216 | tf_op jit(solution)/shard_map/attention_core/pallas_call | solution.py:57
  214.3 14.0 %fusion.40 = (f32[512]{0:T(512)S(1)}, bf16[512,2048]{1,0:T(8,128)(2,1)S(1)}) fusion(bf16[512,4096]{1,0:T(8,128)(2,1)} %attention_core.5, bf16[4096,2048]{1,0:T(8,128)(2,1)} %bitcast.132, bf16[512,2048]{1,0:T(8,128)(2,1)S(1)} %bitcast.127), kind=kOutput, calls=%fused_computation.54 | convolution fusion | flops 8596226048 | bytes 25167872 | tf_op jit(solution)/shard_map/dot_general | solution.py:73
  228.3 1.3 copy-done
  229.6 1.9 fusion.42
  231.6 1.3 slice_bitcast_fusion.2
  232.9 1.9 compare_reduce_fusion
  234.8 0.2 convolution_convert_fusion.2
  235.2 0.8 broadcast_select_fusion.1.slot_ref
  236.0 54.7 %all-gather.13.cloned.1.call-done = bf16[8192,2048]{1,0:T(8,128)(2,1)} async-done(((bf16[256,2048]{1,0:T(8,128)(2,1)}), bf16[8192,2048]{1,0:T(8,128)(2,1)}) %all-gather.13.cloned.1.call-update) | async-done | bytes 33554448 | tf_op jit(solution)/shard_map/all_gather | solution.py:211
  290.7 45.1 %pick_rows.2.x_ref = bf16[4,32,48,2048]{3,2,1,0:T(8,128)(2,1)} custom-call(s32[32,4,512]{2,1,0:T(4,128)} %broadcast_select_fusion.1.slot_ref, bf16[32,256,2048]{2,1,0:T(8,128)(2,1)} %bitcast.121, bf16[32,256,2048]{2,1,0:T(8,128)(2,1)} %bitcast.122), custom_call_target="tpu_custom_call" | custom-call | flops 12884901888 | bytes 92274688 | tf_op jit(solution)/shard_map/pick_rows/pallas_call | solution.py:95
  335.8 69.9 %expert_ffn.2 = bf16[32,4,48,2048]{3,2,1,0:T(8,128)(2,1)} custom-call(bf16[4,32,48,2048]{3,2,1,0:T(8,128)(2,1)} %pick_rows.2.x_ref, bf16[4,2048,768]{2,1,0:T(8,128)(2,1)} %wg_ref.3, bf16[4,2048,768]{2,1,0:T(8,128)(2,1)} %wu_ref.3, bf16[4,768,2048]{2,1,0:T(8,128)(2,1)} %wd_ref.3), custom_call_target="tpu_custom_call" | custom-call | flops 57982058496 | bytes 88080384 | tf_op jit(solution)/shard_map/expert_ffn/pallas_call | solution.py:125
  405.7 82.6 %all-gather.15.cloned.1.call-done = bf16[16384,2048]{1,0:T(8,128)(2,1)} async-done(((bf16[512,2048]{1,0:T(8,128)(2,1)}), bf16[16384,2048]{1,0:T(8,128)(2,1)}) %all-gather.15.cloned.1.call-update) | async-done | bytes 67108880 | tf_op jit(solution)/shard_map/all_gather | solution.py:211
  488.3 6.9 all-to-all-start
  495.3 0.2 convolution_convert_fusion
  495.6 0.8 broadcast_select_fusion.slot_ref
  496.5 45.9 %pick_rows.3.x_ref = bf16[4,32,48,2048]{3,2,1,0:T(8,128)(2,1)} custom-call(s32[32,4,512]{2,1,0:T(4,128)} %broadcast_select_fusion.slot_ref, bf16[32,512,2048]{2,1,0:T(8,128)(2,1)} %bitcast.28.refs_0_), custom_call_target="tpu_custom_call" | custom-call | flops 12884901888 | bytes 92274688 | tf_op jit(solution)/shard_map/pick_rows/pallas_call | solution.py:95
  542.3 69.9 %expert_ffn.3 = bf16[32,4,48,2048]{3,2,1,0:T(8,128)(2,1)} custom-call(bf16[4,32,48,2048]{3,2,1,0:T(8,128)(2,1)} %pick_rows.3.x_ref, bf16[4,2048,768]{2,1,0:T(8,128)(2,1)} %wg_ref.3, bf16[4,2048,768]{2,1,0:T(8,128)(2,1)} %wu_ref.3, bf16[4,768,2048]{2,1,0:T(8,128)(2,1)} %wd_ref.3), custom_call_target="tpu_custom_call" | custom-call | flops 57982058496 | bytes 88080384 | tf_op jit(solution)/shard_map/expert_ffn/pallas_call | solution.py:125
  612.2 238.5 %all-to-all-done = bf16[32,4,48,2048]{3,2,1,0:T(8,128)(2,1)} async-done(((bf16[32,4,48,2048]{3,2,1,0:T(8,128)(2,1)}), bf16[32,4,48,2048]{3,2,1,0:T(8,128)(2,1)}, u32[]{:S(2)}, u32[]{:S(2)}) %all-to-all-start) | async-done | bytes 25165856 | tf_op jit(solution)/shard_map/all_to_all | solution.py:231
  850.8 6.6 all-to-all-start.1
  857.5 0.1 copy.59
  857.6 2.9 fusion.71
  860.6 0.3 fusion.85
  860.9 0.1 copy.60
  861.0 0.1 copy.61
  861.2 2.5 select_reduce_fusion
  863.7 0.1 copy.62
  864.0 0.1 copy.63
  864.1 0.1 copy.50
  864.2 2.9 fusion.72
  867.1 0.3 fusion.86
  867.4 0.1 copy.51
  867.6 0.1 copy.52
  867.7 2.5 select_reduce_fusion.1
  870.3 0.1 copy.53
  870.5 0.1 copy.54
  870.6 14.7 %fusion.32 = (bf16[512,6144]{0,1:T(8,128)(2,1)}, bf16[512,6144]{0,1:T(8,128)(2,1)}, bf16[512,6144]{0,1:T(8,128)(2,1)}, bf16[512,6144]{0,1:T(8,128)(2,1)}, bf16[5...) fusion(bf16[512,128]{0,1:T(8,128)(2,1)S(1)} %copy.62, s32[512,128]{0,1:T(8,128)S(1)} %copy.60, s32[6144]{0:T(1024)S(1)} %eq.109, ...), kind=kLoop, calls=%fused_computation.35 | loop fusion | flops 25165824 | bytes 39084032 | tf_op jit(solution)/shard_map/convert_element_type | solution.py:175
  885.3 46.9 %fusion = f32[1536,2048]{1,0:T(8,128)S(1)} fusion(bf16[6144,2048]{1,0:T(8,128)(2,1)} %bitcast.29, bf16[512,6144]{0,1:T(8,128)(2,1)} %get-tuple-element.31, bf16[512,6144]{0,1:T(8,128)(2,1)} %get-tuple-element.30, bf16[512,6144]{0,1:T(8,128)(2,1)} %get-tuple-element.32), kind=kOutput, calls=%fused_computation | convolution fusion | flops 38711328768 | bytes 56623104 | tf_op jit(solution)/shard_map/dot_general | solution.py:232
  932.2 2.7 fusion.68
  934.9 278.1 %all-to-all-done.1 = bf16[32,4,48,2048]{3,2,1,0:T(8,128)(2,1)} async-done(((bf16[32,4,48,2048]{3,2,1,0:T(8,128)(2,1)}), bf16[32,4,48,2048]{3,2,1,0:T(8,128)(2,1)}, u32[]{:S(2)}, u32[]{:S(2)}) %all-to-all-start.1) | async-done | bytes 25165856 | tf_op jit(solution)/shard_map/all_to_all | solution.py:231
  1213.0 46.9 %fusion.6 = f32[1536,2048]{1,0:T(8,128)S(1)} fusion(bf16[6144,2048]{1,0:T(8,128)(2,1)} %bitcast.38, bf16[512,6144]{0,1:T(8,128)(2,1)} %get-tuple-element.15, bf16[512,6144]{0,1:T(8,128)(2,1)} %get-tuple-element.16, bf16[512,6144]{0,1:T(8,128)(2,1)} %get-tuple-element.14), kind=kOutput, calls=%fused_computation.6 | convolution fusion | flops 38711328768 | bytes 56623104 | tf_op jit(solution)/shard_map/dot_general | solution.py:232
  1259.9 3.0 fusion.69
  (48 shorter events, 1.2 us)
Async XLA Ops:
  7.2 224.4 %all-gather.9.cloned.1.call-start = ((), (), s32[]{:S(2)}) async-start(), calls=%async_computation.2 | async-start | bytes 1081344 | tf_op jit(solution)/shard_map/all_gather | solution.py:196
  8.0 228.0 %all-gather.11.cloned.1.call-start = ((), (), s32[]{:S(2)}) async-start(), calls=%async_computation.3 | async-start | bytes 34603008 | tf_op jit(solution)/shard_map/all_gather | solution.py:211
  9.6 13.3 %copy-start.7 = (bf16[1,512,2048]{2,1,0:T(8,128)(2,1)S(1)}, bf16[1,512,2048]{2,1,0:T(8,128)(2,1)}, u32[]{:S(2)}) copy-start(bf16[1,512,2048]{2,1,0:T(8,128)(2,1)} %param.13) | copy-start | bytes 6291460
  9.6 13.3 %copy-start.11 = (f32[2048]{0:T(1024)S(1)}, f32[2048]{0:T(1024)}, u32[]{:S(2)}) copy-start(f32[2048]{0:T(1024)} %param.17) | copy-start | bytes 24580
  59.9 12.1 copy-start.9
  71.0 1.0 copy-start.2
  73.4 217.3 %all-gather.13.cloned.1.call-start = ((), (), s32[]{:S(2)}) async-start(), calls=%async_computation.4 | async-start | bytes 34603008 | tf_op jit(solution)/shard_map/all_gather | solution.py:211
  140.0 1.0 copy-start.4
  140.0 2.6 copy-start.6
  142.3 346.0 %all-gather.15.cloned.1.call-start = ((), (), s32[]{:S(2)}) async-start(), calls=%async_computation.5 | async-start | bytes 69206016 | tf_op jit(solution)/shard_map/all_gather | solution.py:211
  228.3 1.4 copy-start
  488.3 362.4 %all-to-all-start = ((bf16[32,4,48,2048]{3,2,1,0:T(8,128)(2,1)}), bf16[32,4,48,2048]{3,2,1,0:T(8,128)(2,1)}, u32[]{:S(2)}, u32[]{:S(2)}) async-start(bf16[32,4,48,2048]{3,2,1,0:T(8,128)(2,1)} %expert_ffn.2), calls=%async_computation | async-start | bytes 50331648 | tf_op jit(solution)/shard_map/all_to_all | solution.py:231
  612.2 245.3 %copy-start.8 = (s32[2,512,8]{1,2,0:T(8,128)S(1)}, s32[2,512,8]{1,2,0:T(8,128)}, u32[]{:S(2)}) copy-start(s32[2,512,8]{1,2,0:T(8,128)} %param.15) | copy-start | bytes 98308
  612.2 248.8 %copy-start.10 = (f32[2,512,8]{1,2,0:T(8,128)S(1)}, f32[2,512,8]{1,2,0:T(8,128)}, u32[]{:S(2)}) copy-start(f32[2,512,8]{1,2,0:T(8,128)} %param.16) | copy-start | bytes 98308
  850.8 362.2 %all-to-all-start.1 = ((bf16[32,4,48,2048]{3,2,1,0:T(8,128)(2,1)}), bf16[32,4,48,2048]{3,2,1,0:T(8,128)(2,1)}, u32[]{:S(2)}, u32[]{:S(2)}) async-start(bf16[32,4,48,2048]{3,2,1,0:T(8,128)(2,1)} %expert_ffn.3), calls=%async_computation.1 | async-start | bytes 50331648 | tf_op jit(solution)/shard_map/all_to_all | solution.py:231
  885.3 46.9 %copy-start.3 = (bf16[256,2048]{1,0:T(8,128)(2,1)S(1)}, bf16[256,2048]{1,0:T(8,128)(2,1)}, u32[]{:S(2)}) copy-start(bf16[256,2048]{1,0:T(8,128)(2,1)} %copy-done.2) | copy-start | bytes 3145732
  885.3 46.9 %copy-start.5 = (bf16[256,2048]{1,0:T(8,128)(2,1)S(1)}, bf16[256,2048]{1,0:T(8,128)(2,1)}, u32[]{:S(2)}) copy-start(bf16[256,2048]{1,0:T(8,128)(2,1)} %copy-done.4) | copy-start | bytes 3145732
  1213.0 46.9 %copy-start.1 = (bf16[512,2048]{1,0:T(8,128)(2,1)S(1)}, bf16[512,2048]{1,0:T(8,128)(2,1)}, u32[]{:S(2)}) copy-start(bf16[512,2048]{1,0:T(8,128)(2,1)} %copy-done) | copy-start | bytes 6291460
Sparse Core Ops, SparseCore 0:
  10.1 35.9 all-gather.8
  73.5 107.0 all-gather.10
  183.2 107.4 all-gather.12
  293.2 195.0 all-gather.14

commit v3 on v2

--- a/solution.py
+++ b/solution.py
@@ -11,6 +11,8 @@
 VMEM_MAX = 60 * 1024 * 1024
 F32 = jnp.float32
 BF16 = jnp.bfloat16
+MESH = pl.DeviceIdType.MESH
+CORES = 2
 
 
 def rms_norm(values, norm_gain):
@@ -166,14 +168,213 @@
     return jnp.where(mask, rank, -1)
 
 
-def home_select(ids, gates, num_exp, cap):
-    hit = ids[:, :, None] == jnp.arange(num_exp, dtype=jnp.int32)[None, None, :]
-    mask = jnp.any(hit, axis=1)
-    gate = jnp.sum(jnp.where(hit, gates[:, :, None], 0.0), axis=1)
-    rank = jnp.where(mask, ranks_of(mask, 0), -1)
-    here = rank[:, :, None] == jnp.arange(cap, dtype=jnp.int32)[None, None, :]
-    parts = [jnp.where(here, g.astype(F32)[:, :, None], 0.0).astype(BF16).reshape(ids.shape[0], num_exp * cap) for g in split3(gate)]
-    return jnp.concatenate(parts, axis=0)
+def sources_select(ids, gates, experts):
+    hit = ids[:, None] == experts[None, :, None, None]
+    mask = jnp.any(hit, axis=2)
+    gate = jnp.sum(jnp.where(hit, gates[:, None], 0.0), axis=2)
+    srcs, exps, toks = mask.shape
+    rank = ranks_of(mask.reshape(srcs * exps, toks), 1).reshape(srcs, exps, toks)
+    return jnp.where(mask, rank, -1), gate
+
+
+def place():
+    ep = lax.axis_index('ep')
+    return lax.div(ep, CORES), lax.rem(ep, CORES), lax.axis_index('sub')
+
+
+def exchange_copies(el, er, rl, rr, send, recv, own):
+    nx, _, ny = el.shape[:3]
+    x, c, y = place()
+    copies = []
+    for dc in range(CORES):
+        for dy in range(ny):
+            if dc or dy:
+                c2, y2, n = lax.rem(c + dc, CORES), lax.rem(y + dy, ny), len(copies)
+                copies.append(pltpu.make_async_remote_copy(
+                    src_ref=el.at[:, c2, y2], dst_ref=rl.at[c * ny + y], send_sem=send.at[n], recv_sem=recv.at[n],
+                    device_id={'ep': x * CORES + c2, 'sub': y2}, device_id_type=MESH))
+    for dx in range(nx):
+        for dc in range(CORES):
+            if dc or dx:
+                x2, c2, n = lax.rem(x + dx, nx), lax.rem(c + dc, CORES), len(copies)
+                copies.append(pltpu.make_async_remote_copy(
+                    src_ref=er.at[x2, c2], dst_ref=rr.at[x * CORES + c], send_sem=send.at[n], recv_sem=recv.at[n],
+                    device_id={'ep': x2 * CORES + c2, 'sub': y}, device_id_type=MESH))
+    local = [pltpu.make_async_copy(el.at[:, c, y], rl.at[c * ny + y], own.at[0]),
+             pltpu.make_async_copy(er.at[x, c], rr.at[x * CORES + c], own.at[1])]
+    return copies, local
+
+
+def greet(peers):
+    barrier = pltpu.get_barrier_semaphore()
+    for ep, sub in peers:
+        pl.semaphore_signal(barrier, inc=1, device_id={'ep': ep, 'sub': sub}, device_id_type=MESH)
+    pl.semaphore_wait(barrier, len(peers))
+
+
+def greet_exchange(nx, ny):
+    x, c, y = place()
+    peers = [(x * CORES + lax.rem(c + dc, CORES), lax.rem(y + dy, ny)) for dc in range(CORES) for dy in range(ny) if dc or dy]
+    peers += [(lax.rem(x + dx, nx) * CORES + lax.rem(c + dc, CORES), y) for dc in range(CORES) for dx in range(1, nx)]
+    greet(peers)
+
+
+def exchange_kernel(el, er, rl, rr, send, recv, own):
+    greet_exchange(el.shape[0], el.shape[2])
+    copies, local = exchange_copies(el, er, rl, rr, send, recv, own)
+    for copy in copies + local:
+        copy.start()
+    for copy in copies + local:
+        copy.wait()
+
+
+def exchange_ffn_kernel(el, er, slots, rows, w_gate, w_up, w_down, rl, rr, picked, next_l, next_r, send, recv, own):
+    greet_exchange(el.shape[0], el.shape[2])
+    copies, local = exchange_copies(el, er, rl, rr, send, recv, own)
+    for copy in copies + local:
+        copy.start()
+    exps, srcs, cap, dim = picked.shape
+    toks = rows.shape[1]
+    ff = w_gate.shape[-1]
+    pltpu.emit_pipeline(
+        pick_kernel, grid=(srcs,),
+        in_specs=[pl.BlockSpec((1, exps, toks), lambda s: (s, 0, 0)), pl.BlockSpec((1, toks, dim), lambda s: (s, 0, 0))],
+        out_specs=[pl.BlockSpec((exps, 1, cap, dim), lambda s: (0, s, 0, 0))],
+    )(slots, rows, picked)
+    step = 8
+    half = dim // 2
+    pltpu.emit_pipeline(
+        ffn_kernel, grid=(exps, srcs // step),
+        in_specs=[
+            pl.BlockSpec((1, step, cap, dim), lambda e, s: (e, s, 0, 0)),
+            pl.BlockSpec((1, dim, ff), lambda e, s: (e, 0, 0)),
+            pl.BlockSpec((1, dim, ff), lambda e, s: (e, 0, 0)),
+            pl.BlockSpec((1, ff, dim), lambda e, s: (e, 0, 0)),
+        ],
+        out_specs=[pl.BlockSpec((step, 1, cap, half), lambda e, s: (s, e, 0, 0))] * 2,
+    )(picked, w_gate, w_up, w_down, next_l, next_r)
+    for copy in copies + local:
+        copy.wait()
+
+
+ANY = pl.BlockSpec(memory_space=pl.ANY)
+
+
+def exchange(el, er, collective_id, expert_work=None):
+    nx, _, ny, rows, width = el.shape
+    shapes = [jax.ShapeDtypeStruct((CORES * ny, nx, rows, width), BF16), jax.ShapeDtypeStruct((nx * CORES, ny, rows, width), BF16)]
+    args = [el, er]
+    kernel = exchange_kernel
+    if expert_work is not None:
+        slots, gathered, w_gate, w_up, w_down, cap = expert_work
+        srcs, exps, _ = slots.shape
+        dim = gathered.shape[-1]
+        args += [slots, gathered, w_gate, w_up, w_down]
+        shapes += [jax.ShapeDtypeStruct((exps, srcs, cap, dim), BF16)] + [jax.ShapeDtypeStruct((srcs, exps, cap, dim // 2), BF16)] * 2
+        kernel = exchange_ffn_kernel
+    n = CORES * (nx + ny) - 2
+    return pl.pallas_call(
+        kernel,
+        out_shape=shapes,
+        in_specs=[ANY] * len(args),
+        out_specs=[ANY] * len(shapes),
+        scratch_shapes=[pltpu.SemaphoreType.DMA((n,)), pltpu.SemaphoreType.DMA((n,)), pltpu.SemaphoreType.DMA((2,))],
+        compiler_params=pltpu.CompilerParams(collective_id=collective_id, has_side_effects=True, vmem_limit_bytes=VMEM_MAX),
+        cost_estimate=pl.CostEstimate(flops=10 ** 11, bytes_accessed=10 ** 8, transcendentals=0),
+        name="exchange_rows" if expert_work is None else "exchange_rows_experts",
+    )(*args)
+
+
+def combine_kernel(rl, rr, slot_l, gate_l, slot_r, gate_r, cl, cr, buf_l, buf_r, acc_l, acc_r, load, send_l, send_r, recv_l, recv_r, own):
+    nx, ny = rl.shape[1], rr.shape[1]
+    x, c, y = place()
+    cap_rows = rl.shape[2]
+
+    def load_l(i):
+        return pltpu.make_async_copy(rl.at[:, lax.rem(x + i, nx)], buf_l, load.at[0])
+
+    def load_r(i):
+        return pltpu.make_async_copy(rr.at[:, lax.rem(y + i, ny)], buf_r, load.at[1])
+
+    def send_left(i):
+        x2 = lax.rem(x + i, nx)
+        return pltpu.make_async_remote_copy(src_ref=acc_l.at[i], dst_ref=cl.at[x], send_sem=send_l.at[i], recv_sem=recv_l.at[i], device_id={'ep': x2 * CORES + c, 'sub': y}, device_id_type=MESH)
+
+    def send_right(i):
+        y2 = lax.rem(y + i, ny)
+        return pltpu.make_async_remote_copy(src_ref=acc_r.at[i], dst_ref=cr.at[y], send_sem=send_r.at[i], recv_sem=recv_r.at[i], device_id={'ep': x * CORES + c, 'sub': y2}, device_id_type=MESH)
+
+    def weigh(buf, slot_ref, gate_ref, src, acc, i):
+        exps, toks = slot_ref.shape[1:]
+        cap = buf.shape[0] * cap_rows // exps
+        want = lax.broadcasted_iota(jnp.int32, (cap, toks), 0)
+        slots = slot_ref[src]
+        hits = [want == slots[e:e + 1, :] for e in range(exps)]
+        sels = []
+        for part in split3(gate_ref[src]):
+            wide = part.astype(F32)
+            sels.append(jnp.concatenate([jnp.where(hits[e], wide[e:e + 1, :], 0.0).astype(BF16) for e in range(exps)], axis=0))
+        width = acc.shape[-1]
+        chunk = 256
+        for lo in range(0, width, chunk):
+            rows = buf[:, :, lo:lo + chunk].reshape(-1, chunk)
+            hi, mid, low = (lax.dot_general(sel, rows, (((0,), (0,)), ((), ())), preferred_element_type=F32) for sel in sels)
+            acc[i, :, lo:lo + chunk] = hi + (mid + low)
+
+    load_l(1).start()
+    greet([(lax.rem(x + i, nx) * CORES + c, y) for i in range(1, nx)] + [(x * CORES + c, lax.rem(y + i, ny)) for i in range(1, ny)])
+
+    def body(n, carry):
+        i = lax.rem(n, nx)
+        load_r(n).start()
+        load_l(n).wait()
+        weigh(buf_l, slot_l, gate_l, lax.rem(x + n, nx), acc_l, i)
+
+        @pl.when(n < nx)
+        def _():
+            send_left(i).start()
+            load_l(n + 1).start()
+
+        load_r(n).wait()
+        weigh(buf_r, slot_r, gate_r, lax.rem(y + n, ny), acc_r, i)
+
+        @pl.when(n < nx)
+        def _():
+            send_right(i).start()
+
+        return carry
+
+    lax.fori_loop(1, nx + 1, body, 0)
+    mine = [pltpu.make_async_copy(acc_l.at[0], cl.at[x], own.at[0]), pltpu.make_async_copy(acc_r.at[0], cr.at[y], own.at[1])]
+    for copy in mine:
+        copy.start()
+    for i in range(1, nx):
+        send_left(i).wait()
+        send_right(i).wait()
+    for copy in mine:
+        copy.wait()
+
+
+def combine(rl, rr, left, right, collective_id):
+    nx, ny = rl.shape[1], rr.shape[1]
+    rows, width = rl.shape[2:]
+    toks = left[0].shape[-1]
+    vmem = pl.BlockSpec(memory_space=pltpu.VMEM)
+    dma = lambda n: pltpu.SemaphoreType.DMA((n,))
+    return pl.pallas_call(
+        combine_kernel,
+        out_shape=[jax.ShapeDtypeStruct((n, toks, width), F32) for n in (nx, ny)],
+        in_specs=[ANY, ANY, vmem, vmem, vmem, vmem],
+        out_specs=[ANY, ANY],
+        scratch_shapes=[
+            pltpu.VMEM((rl.shape[0], rows, width), BF16), pltpu.VMEM((rr.shape[0], rows, width), BF16),
+            pltpu.VMEM((nx, toks, width), F32), pltpu.VMEM((ny, toks, width), F32),
+            dma(2), dma(nx), dma(ny), dma(nx), dma(ny), dma(2),
+        ],
+        compiler_params=pltpu.CompilerParams(collective_id=collective_id, has_side_effects=True, vmem_limit_bytes=VMEM_MAX),
+        cost_estimate=pl.CostEstimate(flops=10 ** 11, bytes_accessed=10 ** 8, transcendentals=0),
+        name="combine_rows",
+    )(rl, rr, *left, *right)
 
 
 def solution(mesh):
@@ -193,7 +394,10 @@
         cap = 3 * top_k * tok_count // (2 * num_exp)
         first_exp = lax.axis_index(axes) * exp_local
 
+        nx, ny = ep_size // CORES, sub_size
+        x, c, y = place()
         ids_all = lax.all_gather(jnp.swapaxes(route_idx, 1, 2), axes, axis=0)
+        gates_all = lax.all_gather(jnp.swapaxes(route_gate, 1, 2), axes, axis=0)
 
         weights = (attn_norm, w_query, w_key, w_value, w_out)
         hiddens, gathered = [], []
@@ -213,27 +417,27 @@
             hiddens.append(jnp.concatenate(parts, axis=0) if ranges > 1 else parts[0])
             gathered.append(blocks)
 
-        expert_outs = []
-        for mb, pieces in ((0, 1), (1, 1)):
-            slots = slots_here(ids_all[:, mb], first_exp, exp_local)
-            picked = pick_rows(slots, gathered[mb], cap)
-            expert_outs.append(expert_ffn(picked, w_gate, w_up, w_down, pieces))
-            if mb == 0:
-                expert_outs[0], gathered[1] = lax.optimization_barrier((expert_outs[0], gathered[1]))
-
+        def grid_of(t):
+            return t.reshape(nx, CORES, ny, exp_local * cap, model_dim // 2)
+
+        def selects(mb):
+            ids = ids_all.reshape(nx, CORES, ny, 2, top_k, tok_count)
+            gates = gates_all.reshape(nx, CORES, ny, 2, top_k, tok_count)
+            in_column = x * (CORES * ny * exp_local) + jnp.arange(CORES * ny * exp_local, dtype=jnp.int32)
+            in_row = (jnp.arange(ep_size, dtype=jnp.int32)[:, None] * (ny * exp_local) + y * exp_local + jnp.arange(exp_local, dtype=jnp.int32)[None, :]).reshape(-1)
+            left = sources_select(ids[:, c, y, mb], gates[:, c, y, mb], in_column)
+            right = sources_select(ids[x, c, :, mb], gates[x, c, :, mb], in_row)
+            return left, right
+
+        slots = [slots_here(ids_all[:, mb], first_exp, exp_local) for mb in range(2)]
+        first = expert_ffn(pick_rows(slots[0], gathered[0], cap), w_gate, w_up, w_down, 2)
+        rows_l, rows_r, _, *second = exchange(*map(grid_of, first), 0, (slots[1], gathered[1][0], w_gate, w_up, w_down, cap))
+        sums = [combine(rows_l, rows_r, *selects(0), 1)]
+        sums.append(combine(*exchange(*map(grid_of, second), 2), *selects(1), 3))
         outs = []
-        for mb, tokens in enumerate((input_a, input_b)):
-            select = home_select(route_idx[mb], route_gate[mb], num_exp, cap)
-            pieces = []
-            lo = 0
-            for piece in expert_outs[mb]:
-                width = piece.shape[-1]
-                returned = lax.all_to_all(piece, axes, 0, 0, tiled=True).reshape(num_exp * cap, width)
-                sums = jnp.dot(select, returned, preferred_element_type=F32).reshape(3, tok_count, width)
-                moe_sum = sums[0] + (sums[1] + sums[2])
-                pieces.append((hiddens[mb][:, lo:lo + width].astype(F32) + moe_sum).astype(BF16))
-                lo += width
-            outs.append((jnp.concatenate(pieces, axis=1) if len(pieces) > 1 else pieces[0]).reshape(tokens.shape))
+        for hidden, (cl, cr), tokens in zip(hiddens, sums, (input_a, input_b)):
+            moe_sum = jnp.concatenate([jnp.sum(cl, axis=0), jnp.sum(cr, axis=0)], axis=1)
+            outs.append((hidden.astype(F32) + moe_sum).astype(BF16).reshape(tokens.shape))
         return outs[0], outs[1]
 
     return jax.shard_map(device_body, mesh=mesh, in_specs=(tok_spec, tok_spec, route_spec, route_spec, P(), P(), P(), P(), P(), P(), exp_spec, exp_spec, exp_spec), out_specs=(tok_spec, tok_spec), check_vma=False)

time: 1280 us -> 1130 us (0.88)
  the two profiles are of different devices: /device:TPU:126 before, /device:TPU:97 now
where the time goes in v3:
time: 1130 us; the launch traced here: 1120 us
  Pallas kernels  683 us (60%)
  waiting for transfers between devices  198 us (18%)
  matrix products  170 us (15%)
  other arithmetic  49.2 us (4%)
  between operations  14.6 us (1%)
    pallas_call x2, Pallas kernels, exchange(): pl.pallas_call(kernel, out_shape=shapes, in_specs=[ANY] * len(args), out_...  280 us
    pallas_call x2, Pallas kernels, combine(): pl.pallas_call(combine_kernel, out_shape=[jax.ShapeDtypeStruct((n, toks,...  232 us
    all_gather x3, waiting for transfers between devices, device_body(): blocks.append(lax.all_gather(after, axes, axis=0))  196 us
    dot_general x9, matrix products, attention_rows(): jnp.einsum('sd,dhc->hsc', normed, w, preferred_element_type=F32)  132 us
    pallas_call x1, Pallas kernels, expert_ffn(): pl.pallas_call(ffn_kernel, grid=(exps, srcs // step), out_shape=[jax.Shap...  70.2 us
    pallas_call x3, Pallas kernels, attention_core(): pl.pallas_call(functools.partial(attn_kernel, head_dim ** (-0.5), len(ks)...  56.2 us
    pallas_call x1, Pallas kernels, pick_rows(): pl.pallas_call(pick_kernel, grid=(srcs,), out_shape=jax.ShapeDtypeStruct(...  45 us
    dot_general x3, matrix products, attention_rows(): jnp.dot(context, w_out.reshape(-1, w_out.shape[-1]), preferred_element_ty...  36.3 us
  transfers between devices with their start and end apart: 5, of which 3 were waited for; matrix products, arithmetic and copies ran while one was open for 17% of the time, Pallas kernels for 15%

profile of v3, /device:TPU:97, one launch (start us, length us, event | category | flops | bytes accessed | tf_op | source)
XLA Modules:
  0.0 1124.5 jit_solution(15485775467564691467)
XLA Ops:
  7.3 0.7 all-gather.11.cloned.1.call-update
  8.1 0.7 all-gather.19.cloned.1.call-update
  8.9 1.5 fusion.48
  10.4 1.3 slice_bitcast_fusion
  11.7 12.9 %convert_bitcast_fusion.6.refs_1_.refs_2_ = bf16[32,256,128]{2,1,0:T(8,128)(2,1)} fusion(bf16[2048,32,128]{2,1,0:T(8,128)(2,1)} %param.20, f32[2048]{0:T(1024)S(1)} %copy-done.11, f32[256]{0:T(256)S(1)} %add_rsqrt_fusion.5, bf16[1,512,2048]{2,1,0:T(8,128)(2,1)S(1)} %copy-done.9), kind=kOutput, calls=%fused_computation.78 | convolution fusion | flops 4298113024 | bytes 19932160 | tf_op jit(solution)/shard_map/sd,dhc->hsc/dot_general | solution.py:72
  24.6 12.8 %convert_bitcast_fusion.7.refs_0_ = bf16[32,256,128]{2,1,0:T(8,128)(2,1)} fusion(bf16[2048,32,128]{2,1,0:T(8,128)(2,1)} %param.19, f32[2048]{0:T(1024)S(1)} %copy-done.11, f32[256]{0:T(256)S(1)} %add_rsqrt_fusion.5, bf16[1,512,2048]{2,1,0:T(8,128)(2,1)S(1)} %copy-done.9), kind=kOutput, calls=%fused_computation.79 | convolution fusion | flops 4298113024 | bytes 19932160 | tf_op jit(solution)/shard_map/sd,dhc->hsc/dot_general | solution.py:72
  37.4 25.5 %convert_bitcast_fusion.8.q_ref = bf16[32,256,128]{2,1,0:T(8,128)(2,1)} fusion(bf16[2048,32,128]{2,1,0:T(8,128)(2,1)} %param.18, f32[2048]{0:T(1024)S(1)} %copy-done.11, f32[256]{0:T(256)S(1)} %add_rsqrt_fusion.5, bf16[1,512,2048]{2,1,0:T(8,128)(2,1)S(1)} %copy-done.9), kind=kOutput, calls=%fused_computation.80 | convolution fusion | flops 4298113024 | bytes 19932160 | tf_op jit(solution)/shard_map/sd,dhc->hsc/dot_general | solution.py:72
  63.0 11.1 attention_core.3
  74.1 11.1 fusion.35
  85.2 1.0 copy-done.4
  86.1 1.3 fusion.37
  87.4 0.3 fusion.45
  87.7 12.9 %convert_bitcast_fusion.3.refs_3_ = bf16[32,256,128]{2,1,0:T(8,128)(2,1)} fusion(bf16[2048,32,128]{2,1,0:T(8,128)(2,1)} %param.20, bf16[256,2048]{1,0:T(8,128)(2,1)S(1)} %slice_bitcast_fusion, f32[256]{0:T(256)S(1)} %add_rsqrt_fusion.3, f32[2048]{0:T(1024)S(1)} %copy-done.11), kind=kOutput, calls=%fused_computation.75 | convolution fusion | flops 4298113024 | bytes 19932160 | tf_op jit(solution)/shard_map/sd,dhc->hsc/dot_general | solution.py:72
  100.6 13.3 %convert_bitcast_fusion.4.refs_1_ = bf16[32,256,128]{2,1,0:T(8,128)(2,1)} fusion(bf16[2048,32,128]{2,1,0:T(8,128)(2,1)} %param.19, bf16[256,2048]{1,0:T(8,128)(2,1)S(1)} %slice_bitcast_fusion, f32[256]{0:T(256)S(1)} %add_rsqrt_fusion.3, f32[2048]{0:T(1024)S(1)} %copy-done.11), kind=kOutput, calls=%fused_computation.76 | convolution fusion | flops 4298113024 | bytes 19932160 | tf_op jit(solution)/shard_map/sd,dhc->hsc/dot_general | solution.py:72
  113.9 12.9 %convert_bitcast_fusion.5.q_ref = bf16[32,256,128]{2,1,0:T(8,128)(2,1)} fusion(bf16[2048,32,128]{2,1,0:T(8,128)(2,1)} %param.18, bf16[256,2048]{1,0:T(8,128)(2,1)S(1)} %slice_bitcast_fusion, f32[256]{0:T(256)S(1)} %add_rsqrt_fusion.3, f32[2048]{0:T(1024)S(1)} %copy-done.11), kind=kOutput, calls=%fused_computation.77 | convolution fusion | flops 4298113024 | bytes 19932160 | tf_op jit(solution)/shard_map/sd,dhc->hsc/dot_general | solution.py:72
  126.7 16.1 %attention_core.4 = bf16[256,4096]{1,0:T(8,128)(2,1)} custom-call(bf16[32,256,128]{2,1,0:T(8,128)(2,1)} %convert_bitcast_fusion.5.q_ref, bf16[32,256,128]{2,1,0:T(8,128)(2,1)} %convert_bitcast_fusion.7.refs_0_, bf16[32,256,128]{2,1,0:T(8,128)(2,1)} %convert_bitcast_fusion.4.refs_1_, bf16[32,256,128]{2,1,0:T(8,128)(2,1)} %convert_bitcast_fusion.6.refs_1_.refs_2_, ...), custom_call_target="tpu_custom_call" | custom-call | flops 2147483648 | bytes 12582912 | tf_op jit(solution)/shard_map/attention_core/pallas_call | solution.py:59
  142.8 11.1 fusion.38
  153.9 1.0 copy-done.6
  154.9 1.3 fusion.40
  156.3 0.6 all-gather.13.cloned.1.call-update
  157.0 0.5 fusion.18
  157.5 13.9 %convert_bitcast_fusion.refs_1_ = bf16[32,512,128]{2,1,0:T(8,128)(2,1)} fusion(bf16[2048,32,128]{2,1,0:T(8,128)(2,1)} %param.20, bf16[512,2048]{1,0:T(8,128)(2,1)S(1)} %bitcast.110, f32[2048]{0:T(1024)S(1)} %copy-done.11, f32[512]{0:T(512)S(1)} %add_rsqrt_fusion.1), kind=kOutput, calls=%fused_computation.34 | convolution fusion | flops 8596226048 | bytes 23078912 | tf_op jit(solution)/shard_map/sd,dhc->hsc/dot_general | solution.py:72
  171.4 14.0 %convert_bitcast_fusion.1.refs_0_ = bf16[32,512,128]{2,1,0:T(8,128)(2,1)} fusion(bf16[2048,32,128]{2,1,0:T(8,128)(2,1)} %param.19, bf16[512,2048]{1,0:T(8,128)(2,1)S(1)} %bitcast.111, f32[2048]{0:T(1024)S(1)} %copy-done.11, f32[512]{0:T(512)S(1)} %add_rsqrt_fusion.1), kind=kOutput, calls=%fused_computation.35 | convolution fusion | flops 8596226048 | bytes 23078912 | tf_op jit(solution)/shard_map/sd,dhc->hsc/dot_general | solution.py:72
  185.4 14.1 %convert_bitcast_fusion.2.q_ref = bf16[32,512,128]{2,1,0:T(8,128)(2,1)} fusion(bf16[2048,32,128]{2,1,0:T(8,128)(2,1)} %param.18, bf16[512,2048]{1,0:T(8,128)(2,1)S(1)} %bitcast.112, f32[2048]{0:T(1024)S(1)} %copy-done.11, f32[512]{0:T(512)S(1)} %add_rsqrt_fusion.1), kind=kOutput, calls=%fused_computation.36 | convolution fusion | flops 8596226048 | bytes 23078912 | tf_op jit(solution)/shard_map/sd,dhc->hsc/dot_general | solution.py:72
  199.5 29.0 %attention_core.5 = bf16[512,4096]{1,0:T(8,128)(2,1)} custom-call(bf16[32,512,128]{2,1,0:T(8,128)(2,1)} %convert_bitcast_fusion.2.q_ref, bf16[32,512,128]{2,1,0:T(8,128)(2,1)} %convert_bitcast_fusion.1.refs_0_, bf16[32,512,128]{2,1,0:T(8,128)(2,1)} %convert_bitcast_fusion.refs_1_), custom_call_target="tpu_custom_call" | custom-call | flops 4294967296 | bytes 16777216 | tf_op jit(solution)/shard_map/attention_core/pallas_call | solution.py:59
  228.4 14.2 %fusion.22 = (f32[512]{0:T(512)S(1)}, bf16[512,2048]{1,0:T(8,128)(2,1)S(1)}) fusion(bf16[512,4096]{1,0:T(8,128)(2,1)} %attention_core.5, bf16[4096,2048]{1,0:T(8,128)(2,1)} %bitcast.131, bf16[512,2048]{1,0:T(8,128)(2,1)S(1)} %bitcast.113), kind=kOutput, calls=%fused_computation.28 | convolution fusion | flops 8596226048 | bytes 25167872 | tf_op jit(solution)/shard_map/dot_general | solution.py:75
  242.7 1.3 copy-done
  244.0 1.9 fusion.24
  246.0 0.1 add.181
  246.1 1.3 slice_bitcast_fusion.2
  247.4 1.9 compare_reduce_fusion.4
  249.4 0.2 convolution_convert_fusion.5
  249.6 0.1 reshape.227
  249.8 0.2 convolution_convert_fusion.4
  250.1 0.9 dynamic-slice_bitcast_fusion.5
  251.0 0.9 dynamic-slice_bitcast_fusion.7
  251.9 0.9 dynamic-slice_bitcast_fusion.4
  252.8 0.9 dynamic-slice_bitcast_fusion.6
  253.7 1.7 compare_reduce_fusion
  255.4 1.7 compare_reduce_fusion.1
  257.1 0.2 convolution_convert_fusion.2
  257.4 0.2 convolution_convert_fusion
  257.6 0.2 convolution_convert_fusion.3
  257.9 0.2 convolution_convert_fusion.1
  258.2 0.8 broadcast_select_fusion.5.slot_ref
  259.0 0.8 broadcast_select_fusion.4.slots
  259.8 0.9 broadcast_select_fusion
  260.6 0.9 broadcast_select_fusion.1
  261.5 3.6 fusion.43
  265.1 3.8 all-gather.15.cloned.1.call-done
  268.9 109.4 %all-gather.13.cloned.1.call-done = bf16[8192,2048]{1,0:T(8,128)(2,1)} async-done(((bf16[256,2048]{1,0:T(8,128)(2,1)}), bf16[8192,2048]{1,0:T(8,128)(2,1)}) %all-gather.13.cloned.1.call-update) | async-done | bytes 33554448 | tf_op jit(solution)/shard_map/all_gather | solution.py:415
  378.3 45.0 %pick_rows.1.x_ref = bf16[4,32,48,2048]{3,2,1,0:T(8,128)(2,1)} custom-call(s32[32,4,512]{2,1,0:T(4,128)} %broadcast_select_fusion.5.slot_ref, bf16[32,256,2048]{2,1,0:T(8,128)(2,1)} %bitcast.104, bf16[32,256,2048]{2,1,0:T(8,128)(2,1)} %bitcast.103), custom_call_target="tpu_custom_call" | custom-call | flops 12884901888 | bytes 92274688 | tf_op jit(solution)/shard_map/pick_rows/pallas_call | solution.py:97
  423.4 70.2 %expert_ffn.1 = (bf16[32,4,48,1024]{3,2,1,0:T(8,128)(2,1)}, bf16[32,4,48,1024]{3,2,1,0:T(8,128)(2,1)}) custom-call(bf16[4,32,48,2048]{3,2,1,0:T(8,128)(2,1)} %pick_rows.1.x_ref, bf16[4,2048,768]{2,1,0:T(8,128)(2,1)} %w_gate.1, bf16[4,2048,768]{2,1,0:T(8,128)(2,1)} %w_up.1, bf16[4,768,2048]{2,1,0:T(8,128)(2,1)} %w_down.1), custom_call_target="tpu_custom_call" | custom-call | flops 57982058496 | bytes 88080384 | tf_op jit(solution)/shard_map/expert_ffn/pallas_call | solution.py:127
  493.6 82.4 %all-gather.17.cloned.1.call-done = bf16[16384,2048]{1,0:T(8,128)(2,1)} async-done(((bf16[512,2048]{1,0:T(8,128)(2,1)}), bf16[16384,2048]{1,0:T(8,128)(2,1)}) %all-gather.17.cloned.1.call-update) | async-done | bytes 67108880 | tf_op jit(solution)/shard_map/all_gather | solution.py:415
  576.0 140.0 %exchange_rows_experts.1 = (bf16[8,4,192,1024]{3,2,1,0:T(8,128)(2,1)}, bf16[8,4,192,1024]{3,2,1,0:T(8,128)(2,1)}, bf16[4,32,48,2048]{3,2,1,0:T(8,128)(2,1)}, bf1...) custom-call(bf16[4,2,4,192,1024]{4,3,2,1,0:T(8,128)(2,1)} %bitcast.132, bf16[4,2,4,192,1024]{4,3,2,1,0:T(8,128)(2,1)} %bitcast.133, ...), custom_call_target="tpu_custom_call" | custom-call | flops 99999997952 | bytes 100000000 | tf_op jit(solution)/shard_map/exchange_rows_experts/pallas_call | solution.py:276
  716.0 139.7 %exchange_rows.1 = (bf16[8,4,192,1024]{3,2,1,0:T(8,128)(2,1)}, bf16[8,4,192,1024]{3,2,1,0:T(8,128)(2,1)}) custom-call(bf16[4,2,4,192,1024]{4,3,2,1,0:T(8,128)(2,1)} %bitcast.134, bf16[4,2,4,192,1024]{4,3,2,1,0:T(8,128)(2,1)} %bitcast.135), custom_call_target="tpu_custom_call" | custom-call | flops 99999997952 | bytes 100000000 | tf_op jit(solution)/shard_map/exchange_rows/pallas_call | solution.py:276
  855.7 115.1 %combine_rows.3 = (f32[4,512,1024]{2,1,0:T(8,128)}, f32[4,512,1024]{2,1,0:T(8,128)}) custom-call(bf16[8,4,192,1024]{3,2,1,0:T(8,128)(2,1)} %get-tuple-element.26.rl, bf16[8,4,192,1024]{3,2,1,0:T(8,128)(2,1)} %get-tuple-element.27.rr, s32[4,32,512]{2,1,0:T(8,128)} %get-tuple-element.56.slot_l, f32[4,32,512]{2,1,0:T(8,128)} %get-tuple-element.34.gate_l, ...), custom_call_target="tpu_custom_call" | custom-call | flops 99999997952 | bytes 100000000 | tf_op jit(solution)/shard_map/combine_rows/pallas_call | solution.py:364
  970.9 5.9 reduce_sum.138
  976.8 5.9 reduce_sum.139
  982.6 116.4 %combine_rows.2 = (f32[4,512,1024]{2,1,0:T(8,128)}, f32[4,512,1024]{2,1,0:T(8,128)}) custom-call(bf16[8,4,192,1024]{3,2,1,0:T(8,128)(2,1)} %get-tuple-element.20.rl, bf16[8,4,192,1024]{3,2,1,0:T(8,128)(2,1)} %get-tuple-element.21.rr, s32[4,32,512]{2,1,0:T(8,128)} %get-tuple-element.57.slot_l, f32[4,32,512]{2,1,0:T(8,128)} %get-tuple-element.35.gate_l, ...), custom_call_target="tpu_custom_call" | custom-call | flops 99999997952 | bytes 100000000 | tf_op jit(solution)/shard_map/combine_rows/pallas_call | solution.py:364
  1099.1 5.9 reduce_sum.134
  1105.0 6.0 reduce_sum.135
  1111.0 4.4 fusion.51
  1115.4 2.1 fusion.26
  (43 shorter events, 0.8 us)
Async XLA Ops:
  7.2 4.5 copy-start.9
  7.2 4.5 copy-start.11
  7.2 238.9 %all-gather.11.cloned.1.call-start = ((), (), s32[]{:S(2)}) async-start(), calls=%async_computation | async-start | bytes 1081344 | tf_op jit(solution)/shard_map/all_gather | solution.py:399
  8.0 243.9 %all-gather.19.cloned.1.call-start = ((), (), s32[]{:S(2)}) async-start(), calls=%async_computation.4 | async-start | bytes 1081344 | tf_op jit(solution)/shard_map/all_gather | solution.py:400
  8.8 260.1 %all-gather.15.cloned.1.call-start = ((), (), s32[]{:S(2)}) async-start(), calls=%async_computation.2 | async-start | bytes 34603008 | tf_op jit(solution)/shard_map/all_gather | solution.py:415
  74.1 12.0 %copy-start.10 = (f32[2048]{0:T(1024)S(1)}, f32[2048]{0:T(1024)}, u32[]{:S(2)}) copy-start(f32[2048]{0:T(1024)} %param.22) | copy-start | bytes 24580
  85.1 1.0 copy-start.4
  153.9 1.0 copy-start.6
  154.9 2.1 copy-start.8
  156.2 222.1 %all-gather.13.cloned.1.call-start = ((), (), s32[]{:S(2)}) async-start(), calls=%async_computation.1 | async-start | bytes 34603008 | tf_op jit(solution)/shard_map/all_gather | solution.py:415
  156.9 419.1 %all-gather.17.cloned.1.call-start = ((), (), s32[]{:S(2)}) async-start(), calls=%async_computation.3 | async-start | bytes 69206016 | tf_op jit(solution)/shard_map/all_gather | solution.py:415
  242.7 1.3 copy-start
  1105.0 6.0 copy-start.1
  1111.0 4.4 copy-start.2
  1111.0 4.4 copy-start.3
  1111.0 4.4 copy-start.5
  1111.0 4.4 copy-start.7
Sparse Core Ops, SparseCore 0:
  10.1 41.6 all-gather.10
  53.9 36.7 all-gather.18
  156.4 112.4 all-gather.14
  270.8 107.4 all-gather.12
  380.8 195.0 all-gather.16
